TPU v7x, 32 devices: a whole 2x2x4 slice. The times are simulated.
32 devices in a mesh: dp: 8 (over y, x, core), seq: 4 (over z).
Axes of the slice: x: 2, y: 2, z: 4, core: 2. Of those that a mesh axis runs over, the one named last changes fastest.
Arguments:
- tokens: bfloat16 [8, 1024, 1024], P('dp', 'seq'), may hold values from -6 to 6
- segments: int32 [8, 1024], P('dp'), may hold values from 0 to 6, as said below
- w_qkv: bfloat16 [1024, 3072], P('dp'), may hold values from -0.1875 to 0.1875
- w_attn_out: bfloat16 [1024, 1024], P('dp'), may hold values from -0.1875 to 0.1875
- w_in: bfloat16 [1024, 8192], P('dp'), may hold values from -0.1875 to 0.1875
- w_down: bfloat16 [4096, 1024], P('dp'), may hold values from -0.09375 to 0.09375
- s_qk: float32 [1024], replicated, may hold values from 1 to 1.8
- s_u: float32 [4096], replicated, may hold values from 0.5 to 2
- s_v: float32 [4096], replicated, may hold values from 0.5 to 2
- alpha_attn: float32 [1024], replicated, may hold values from 0.05 to 0.4
- alpha_mlp: float32 [1024], replicated, may hold values from 0.05 to 0.4
- cotangent: bfloat16 [8, 1024, 1024], P('dp', 'seq'), may hold values from -6 to 6
Outputs:
- output: bfloat16 [8, 1024, 1024], P('dp', 'seq')
- grad_tokens: float32 [8, 1024, 1024], P('dp', 'seq')
- grad_w_qkv: float32 [1024, 3072], P(('dp', 'seq'))
- grad_w_attn_out: float32 [1024, 1024], P(('dp', 'seq'))
- grad_w_in: float32 [1024, 8192], P(('dp', 'seq'))
- grad_w_down: float32 [4096, 1024], P(('dp', 'seq'))
- grad_s_qk: float32 [1024], P(('dp', 'seq'))
- grad_s_u: float32 [4096], P(('dp', 'seq'))
- grad_s_v: float32 [4096], P(('dp', 'seq'))
- grad_alpha_attn: float32 [1024], P(('dp', 'seq'))
- grad_alpha_mlp: float32 [1024], P(('dp', 'seq'))
Inputs may be any that keep to these rules, and one draw needn't show every extreme that they name: `segments`: in each sequence ids count documents from 1 at the first token and rise by one at each new document; documents hold 200 to 2000 tokens except where a sequence's end cuts one; each sequence ends in 1 to 199 padding tokens of id 0; in one sequence of each draw every whole document holds exactly 200 tokens and one padding token ends it.
All inputs are finite; a program needn't handle non-finite values.
Results may differ from a plain program's by a relative error of at most 0.019.
Values may be sent and summed in bfloat16 or wider, within the bound.
A program may use at most 192 MiB of HBM per device.

v0:
```python
import math

import jax
import jax.numpy as jnp
from jax import lax
from jax.sharding import PartitionSpec as P

HEADS = 16
HD = 64


EPS = 1e-06
ROPE_BASE = 10000.0
MASKED_SCORE = -1e30


def as_sent(array):

    def short(part):
        return part.astype(jnp.bfloat16) if part.dtype == jnp.float32 else part

    return jax.tree.map(short, array)


def rms_norm(values):
    inverse = lax.rsqrt(jnp.mean(values * values, axis=-1, keepdims=True) + EPS)
    return (values * inverse, inverse)


def rms_back(grad_in, normed, inverse):
    return inverse * (grad_in - normed * jnp.mean(grad_in * normed, axis=-1, keepdims=True))


def contract_rows(left_arr, right_arr):
    return lax.dot_general(
        left_arr, right_arr, (((0,), (0,)), ((), ())), preferred_element_type=jnp.float32
    )


def contract_cols(left_arr, right_arr):
    return lax.dot_general(
        left_arr, right_arr, (((1,), (1,)), ((), ())), preferred_element_type=jnp.float32
    )


def doc_positions(seg_row):
    length = seg_row.shape[0]
    places = jnp.arange(length, dtype=jnp.int32)
    is_start = jnp.concatenate([jnp.ones((1,), dtype=bool), seg_row[1:] != seg_row[:-1]])
    starts = lax.cummax(jnp.where(is_start, places, 0), axis=0)
    return (places - starts).astype(jnp.float32)


def rope_tables(positions, head_dim):
    half_dim = head_dim // 2
    inverse_freq = ROPE_BASE ** (-(jnp.arange(half_dim, dtype=jnp.float32) * 2.0 / head_dim))
    angles = positions[:, None] * inverse_freq[None, :]
    return (jnp.cos(angles)[:, None, :], jnp.sin(angles)[:, None, :])


def rotate(values, cosine, sine_tab):
    half_dim = values.shape[-1] // 2
    low_half = values[..., :half_dim]
    high_half = values[..., half_dim:]
    return jnp.concatenate(
        [low_half * cosine - high_half * sine_tab, high_half * cosine + low_half * sine_tab],
        axis=-1,
    )


def head_prep(head_raw, cosine, sine_tab, head_gain):
    rotated = rotate(head_raw.astype(jnp.float32), cosine, sine_tab)
    head_unit, inverse = rms_norm(rotated)
    return (head_unit, inverse, (head_unit * head_gain).astype(jnp.bfloat16))


def head_back(grad_n, head_unit, inverse, head_gain, cosine, sine_tab):
    grad_rot = rms_back(grad_n * head_gain, head_unit, inverse)
    return rotate(grad_rot, cosine, -sine_tab)


def allowed(seg_row, block_start, block_len):
    query_idx = block_start + jnp.arange(block_len, dtype=jnp.int32)
    key_idx = jnp.arange(seg_row.shape[0], dtype=jnp.int32)
    seg_query = lax.dynamic_slice_in_dim(seg_row, block_start, block_len)
    same_doc = seg_query[:, None] == seg_row[None, :]
    causal = key_idx[None, :] <= query_idx[:, None]
    not_padding = (seg_query[:, None] != 0) | (key_idx[None, :] == query_idx[:, None])
    return causal & same_doc & not_padding


def attend_forward(query_n, key_n, value_b, seg_row, score_scale):
    length, groups, head_dim = query_n.shape
    block_len = min(512, length)
    block_count = length // block_len
    query_blocks = query_n.reshape(block_count, block_len, groups, head_dim)
    starts = jnp.arange(block_count, dtype=jnp.int32) * block_len

    def one_block(block_in):
        query_part, block_start = block_in
        scores = (
            jnp.einsum("qhd,khd->hqk", query_part, key_n, preferred_element_type=jnp.float32)
            * score_scale
        )
        mask_ok = allowed(seg_row, block_start, block_len)
        scores = jnp.where(mask_ok[None], scores, MASKED_SCORE)
        row_max = jnp.max(scores, axis=-1, keepdims=True)
        weights_exp = jnp.exp(scores - row_max)
        row_total = jnp.sum(weights_exp, axis=-1, keepdims=True)
        attn_probs = (weights_exp / row_total).astype(jnp.bfloat16)
        attn_part = jnp.einsum(
            "hqk,khd->qhd", attn_probs, value_b, preferred_element_type=jnp.float32
        )
        return (attn_part.astype(jnp.bfloat16), (row_max + jnp.log(row_total))[..., 0])

    attn_mixed, log_sums = lax.map(one_block, (query_blocks, starts))
    return (attn_mixed.reshape(length, groups * head_dim), log_sums)


def attend_backward(query_n, key_n, value_b, grad_attn, log_sums, seg_row, score_scale):
    length, groups, head_dim = query_n.shape
    block_len = min(512, length)
    block_count = length // block_len
    query_blocks = query_n.reshape(block_count, block_len, groups, head_dim)
    grad_blocks = grad_attn.reshape(block_count, block_len, groups, head_dim)
    starts = jnp.arange(block_count, dtype=jnp.int32) * block_len

    def one_block(accums, block_in):
        key_acc, value_acc = accums
        query_part, grad_part, lse_part, block_start = block_in
        scores = (
            jnp.einsum("qhd,khd->hqk", query_part, key_n, preferred_element_type=jnp.float32)
            * score_scale
        )
        mask_ok = allowed(seg_row, block_start, block_len)
        attn_probs = jnp.where(mask_ok[None], jnp.exp(scores - lse_part[..., None]), 0.0)
        grad_probs = jnp.einsum(
            "qhd,khd->hqk", grad_part, value_b, preferred_element_type=jnp.float32
        )
        delta_row = jnp.sum(grad_probs * attn_probs, axis=-1, keepdims=True)
        grad_scores = (attn_probs * (grad_probs - delta_row)).astype(jnp.bfloat16)
        grad_query = (
            jnp.einsum("hqk,khd->qhd", grad_scores, key_n, preferred_element_type=jnp.float32)
            * score_scale
        )
        key_acc = (
            key_acc
            + jnp.einsum(
                "hqk,qhd->khd", grad_scores, query_part, preferred_element_type=jnp.float32
            )
            * score_scale
        )
        value_acc = value_acc + jnp.einsum(
            "hqk,qhd->khd",
            attn_probs.astype(jnp.bfloat16),
            grad_part,
            preferred_element_type=jnp.float32,
        )
        return ((key_acc, value_acc), grad_query)

    zeros_init = jnp.zeros((length, groups, head_dim), jnp.float32)
    (grad_key, grad_value), grad_query = lax.scan(
        one_block, (zeros_init, zeros_init), (query_blocks, grad_blocks, log_sums, starts)
    )
    return (grad_query.reshape(length, groups, head_dim), grad_key, grad_value)


def body(
    tokens,
    segments,
    w_qkv,
    w_attn_out,
    w_in,
    w_down,
    s_qk,
    s_u,
    s_v,
    alpha_attn,
    alpha_mlp,
    cotangent,
):
    model_width = tokens.shape[-1]
    inputs_b = tokens.reshape(-1, model_width)
    inputs_f = inputs_b.astype(jnp.float32)
    seg_row = segments.reshape(-1)
    seq_count = lax.axis_size("seq")
    dp_count = lax.axis_size("dp")
    head_group = HEADS // seq_count
    group_width = head_group * HD
    offset = lax.axis_index("seq") * group_width
    head_gain = lax.dynamic_slice_in_dim(s_qk, offset, group_width).reshape(head_group, HD)
    score_scale = 1.0 / math.sqrt(HD)
    full_qkv, full_out, full_in, full_down = (
        lax.all_gather(w_qkv, "dp", axis=0, tiled=True),
        lax.all_gather(w_attn_out, "dp", axis=0, tiled=True),
        lax.all_gather(w_in, "dp", axis=0, tiled=True),
        lax.all_gather(w_down, "dp", axis=0, tiled=True),
    )
    projected = jnp.dot(inputs_b, full_qkv, preferred_element_type=jnp.float32).astype(jnp.bfloat16)
    by_heads = lax.all_to_all(
        projected.reshape(-1, 3, model_width), "seq", split_axis=2, concat_axis=0, tiled=True
    )
    length = by_heads.shape[0]
    cosine, sine_tab = rope_tables(doc_positions(seg_row), HD)
    query_unit, query_inv, query_n = head_prep(
        by_heads[:, 0].reshape(length, head_group, HD), cosine, sine_tab, head_gain
    )
    key_unit, key_inv, key_n = head_prep(
        by_heads[:, 1].reshape(length, head_group, HD), cosine, sine_tab, head_gain
    )
    value_b = by_heads[:, 2].reshape(length, head_group, HD)
    attn_mixed, log_sums = attend_forward(query_n, key_n, value_b, seg_row, score_scale)
    attn_pieces = lax.all_to_all(attn_mixed, "seq", split_axis=0, concat_axis=1, tiled=True)
    attn_proj = jnp.dot(attn_pieces, full_out, preferred_element_type=jnp.float32)
    attn_unit, attn_inv = rms_norm(attn_proj)
    hidden, hidden_inv = rms_norm(inputs_f + alpha_attn * (attn_unit - inputs_f))
    hidden_b = hidden.astype(jnp.bfloat16)
    up_gate = jnp.dot(hidden_b, full_in, preferred_element_type=jnp.float32)
    ff_width = s_u.shape[0]
    up_raw = up_gate[:, :ff_width]
    gate_raw = up_gate[:, ff_width:]
    up_val = s_u * up_raw
    gate_val = s_v * gate_raw
    gate_sig = jax.nn.sigmoid(gate_val)
    silu_gate = gate_val * gate_sig
    inner_act = (silu_gate * up_val).astype(jnp.bfloat16)
    down_proj = jnp.dot(inner_act, full_down, preferred_element_type=jnp.float32)
    mlp_unit, mlp_inv = rms_norm(down_proj)
    result, result_inv = rms_norm(hidden + alpha_mlp * (mlp_unit - hidden))
    output = result.astype(jnp.bfloat16).reshape(tokens.shape)
    grad_res = cotangent.reshape(-1, model_width).astype(jnp.float32)
    grad_two = rms_back(grad_res, result, result_inv)
    grad_alpha_mlp = jnp.sum(grad_two * (mlp_unit - hidden), axis=0)
    grad_down_proj = rms_back(alpha_mlp * grad_two, mlp_unit, mlp_inv).astype(jnp.bfloat16)
    grad_w_down = contract_rows(inner_act, grad_down_proj)
    grad_inner = contract_cols(grad_down_proj, full_down)
    grad_up_val = grad_inner * silu_gate
    grad_gate_val = grad_inner * up_val * gate_sig * (1.0 + gate_val * (1.0 - gate_sig))
    grad_s_u = jnp.sum(grad_up_val * up_raw, axis=0)
    grad_s_v = jnp.sum(grad_gate_val * gate_raw, axis=0)
    grad_up_gate = jnp.concatenate([grad_up_val * s_u, grad_gate_val * s_v], axis=1).astype(
        jnp.bfloat16
    )
    grad_w_in = contract_rows(hidden_b, grad_up_gate)
    grad_hidden = (1.0 - alpha_mlp) * grad_two + contract_cols(grad_up_gate, full_in)
    grad_one = rms_back(grad_hidden, hidden, hidden_inv)
    grad_alpha_attn = jnp.sum(grad_one * (attn_unit - inputs_f), axis=0)
    grad_attn_proj = rms_back(alpha_attn * grad_one, attn_unit, attn_inv).astype(jnp.bfloat16)
    grad_w_attn_out = contract_rows(attn_pieces, grad_attn_proj)
    grad_pieces = contract_cols(grad_attn_proj, full_out).astype(jnp.bfloat16)
    grad_heads = lax.all_to_all(
        grad_pieces, "seq", split_axis=1, concat_axis=0, tiled=True
    ).reshape(length, head_group, HD)
    grad_query_n, grad_key_n, grad_value = attend_backward(
        query_n, key_n, value_b, grad_heads, log_sums, seg_row, score_scale
    )
    grad_head_gain = jnp.sum(grad_query_n * query_unit + grad_key_n * key_unit, axis=0)
    grad_query = head_back(grad_query_n, query_unit, query_inv, head_gain, cosine, sine_tab)
    grad_key = head_back(grad_key_n, key_unit, key_inv, head_gain, cosine, sine_tab)
    grad_stack = (
        jnp.stack([grad_query, grad_key, grad_value], axis=1)
        .reshape(length, 3, group_width)
        .astype(jnp.bfloat16)
    )
    grad_qkv = lax.all_to_all(grad_stack, "seq", split_axis=0, concat_axis=2, tiled=True).reshape(
        -1, 3 * model_width
    )
    grad_w_qkv = contract_rows(inputs_b, grad_qkv)
    grad_inputs = (1.0 - alpha_attn) * grad_one + contract_cols(grad_qkv, full_qkv)
    grad_s_qk = lax.dynamic_update_slice_in_dim(
        jnp.zeros((model_width,), jnp.float32), grad_head_gain.reshape(-1), offset, 0
    )
    grad_terms = (
        grad_w_qkv,
        grad_w_attn_out,
        grad_w_in,
        grad_w_down,
        grad_s_qk,
        grad_s_u,
        grad_s_v,
        grad_alpha_attn,
        grad_alpha_mlp,
    )
    shaped = tuple(
        (
            term_arr.reshape(
                (dp_count, seq_count, term_arr.shape[0] // (dp_count * seq_count))
                + term_arr.shape[1:]
            )
            for term_arr in grad_terms
        )
    )
    within = jax.tree.map(
        lambda part: part.astype(jnp.float32),
        lax.psum_scatter(as_sent(shaped), "seq", scatter_dimension=1, tiled=True),
    )
    across = jax.tree.map(
        lambda part: part.astype(jnp.float32),
        lax.psum_scatter(as_sent(within), "dp", scatter_dimension=0, tiled=True),
    )
    shards = tuple((term_arr.reshape(term_arr.shape[2:]) for term_arr in across))
    return (output, grad_inputs.reshape(tokens.shape)) + tuple(shards)


def solution(mesh):
    placed = (
        P("dp", "seq", None),
        P("dp", None),
        P("dp", None),
        P("dp", None),
        P("dp", None),
        P("dp", None),
        P(),
        P(),
        P(),
        P(),
        P(),
        P("dp", "seq", None),
    )
    return jax.shard_map(
        body,
        mesh=mesh,
        in_specs=placed,
        out_specs=(
            P("dp", "seq", None),
            P("dp", "seq", None),
            P(("dp", "seq"), None),
            P(("dp", "seq"), None),
            P(("dp", "seq"), None),
            P(("dp", "seq"), None),
            P(("dp", "seq")),
            P(("dp", "seq")),
            P(("dp", "seq")),
            P(("dp", "seq")),
            P(("dp", "seq")),
        ),
        check_vma=False,
    )
```

profile of v0, /device:TPU:0, one launch (start us, length us, event | category | flops | bytes accessed | tf_op | source)
XLA Modules:
  0.0 1722.5 jit_solution(12970683820882381391)
XLA Ops:
  9.4 48.6 %all-gather.5.cloned.1.call-done = bf16[1024,3072]{1,0:T(8,128)(2,1)} async-done(((bf16[128,3072]{1,0:T(8,128)(2,1)}), bf16[1024,3072]{1,0:T(8,128)(2,1)}) %all-gather.5.cloned.1.call-update) | async-done | bytes 6291472 | tf_op jit(solution)/shard_map/all_gather | solution.py:194
  58.0 4.8 convolution_convert_fusion.3
  66.2 4.6 all-to-all-start
  74.2 45.2 %all-to-all-done = bf16[256,3,1024]{0,1,2:T(4,128)(2,1)S(1)} async-done(((bf16[256,3,1024]{0,1,2:T(4,128)(2,1)}), bf16[256,3,1024]{0,1,2:T(4,128)(2,1)S(1)}, u32[]{:S(2)}, u32[]{:S(2)}) %all-to-all-start) | async-done | bytes 1572896 | tf_op jit(solution)/shard_map/all_to_all | solution.py:200
  135.9 27.1 %while.27 = (s32[]{:T(128)}, bf16[2,512,4,64]{1,3,2,0:T(8,128)(2,1)}, f32[2,4,512]{2,1,0:T(4,128)S(1)}, s32[2]{0:T(128)S(1)}, s32[1024]{0:T(1024)S(1)}, /*index=...) while((s32[]{:T(128)}, ...), condition=%wide.region_7.8_spmd, body=%wide.region_4.7_spmd.sunk | while | flops 565312512 | bytes 33111288 | solution.py:116
  169.5 13.9 all-to-all-done.1
  187.5 9.0 fusion.72
  202.0 33.4 %all-gather.11.cloned.1.call-done = bf16[4096,1024]{1,0:T(8,128)(2,1)} async-done(((bf16[512,1024]{1,0:T(8,128)(2,1)}), bf16[4096,1024]{1,0:T(8,128)(2,1)}) %all-gather.11.cloned.1.call-update) | async-done | bytes 8388624 | tf_op jit(solution)/shard_map/all_gather | solution.py:197
  235.4 6.5 multiply_reduce_fusion.11
  245.9 9.2 multiply_reduce_fusion.1
  256.8 12.7 multiply_reduce_fusion.8
  275.4 4.8 all-to-all-start.2
  280.2 14.9 all-to-all-done.2
  299.0 62.1 %while.28 = (s32[]{:T(128)}, f32[1024,4,64]{0,2,1:T(8,128)S(1)}, f32[1024,4,64]{0,2,1:T(8,128)}, f32[2,512,4,64]{1,0,3,2:T(2,128)}, bf16[2,512,4,64]{1,3,2,0:T(8...) while((s32[]{:T(128)}, f32[1024,4,64]{0,2,1:T(8,128)S(1)}, ...), condition=%wide.region_18.19_spmd.clone, body=%wide.region_16.18_spmd.clone.sunk | while | flops 1378221056 | bytes 82910512 | solution.py:162
  308.6 4.8 multiply_reduce_fusion.17
  319.7 10.4 dynamic_update_slice.24
  339.7 4.8 multiply_reduce_fusion.17
  350.7 10.4 dynamic_update_slice.24
  373.8 4.6 all-to-all-start.3
  380.5 7.2 convolution_convert_fusion.1
  387.7 10.4 convolution_convert_fusion
  398.2 28.0 %all-to-all-done.3 = bf16[1024,3,256]{2,1,0:T(4,128)(2,1)} async-done(((bf16[1024,3,256]{2,1,0:T(4,128)(2,1)}), bf16[1024,3,256]{2,1,0:T(4,128)(2,1)}, u32[]{:S(2)}, u32[]{:S(2)}) %all-to-all-start.3) | async-done | bytes 1572896 | tf_op jit(solution)/shard_map/all_to_all | solution.py:265
  428.7 5.5 convolution_convert_fusion.2
  435.5 1101.0 %all-reduce.19.cloned.1.call-done = (bf16[8,4,32,3072]{3,2,1,0:T(8,128)(2,1)}, bf16[8,4,32,1024]{3,2,1,0:T(8,128)(2,1)}, bf16[8,4,32,8192]{3,2,1,0:T(8,128)(2,1)}, bf16[8,4,128,1024]{3,2,1,0:T(8,128)(2,1)}) async-done(((bf16[8,4,32,3072]{3,2,1,0:T(8,128)(2,1)}, bf16[8,4,32,1024]{3,2,1,0:T(8,128)(2,1)}, bf16[8,4,32,8192]{3,2,1,0:T(8,128)(2,1)}, bf16[8,4,128,1024]{3,2,1,0:T(8,128)(2,1)}), ...) | async-done | bytes 33554448
  1542.4 3.8 constant_dynamic-slice_fusion.10
  1546.5 5.3 constant_dynamic-slice_fusion.11
  1553.7 16.8 all-reduce.15
  1573.8 22.4 %all-reduce.14 = (bf16[8,1,32]{2,1,0:T(2,128)(2,1)S(1)}, bf16[8,1,128]{2,1,0:T(2,128)(2,1)S(1)}, bf16[8,1,128]{2,1,0:T(2,128)(2,1)S(1)}, bf16[8,1,32]{2,1,0:T(2,128)(2,1)S(1)}, bf16[8,1,32]{2,1,0:T(2,128)(2,1)S(1)}) all-reduce(bf16[8,1,32]{2,1,0:T(2,128)(2,1)S(1)} %copy.111, ...), channel_id=11, replica_groups=mesh['dp'=8,'seq'=4] {'dp'}, use_global_device_ids=true, to_apply=%region_31.32.clone | all-reduce | flops 2816 | bytes 11264
  1602.0 5.7 fusion.50
  1609.2 5.4 reduce-scatter.17.cloned.1.call-done
  1616.3 42.7 %reduce-scatter.23.cloned.1.call-done = bf16[1,1,128,1024]{3,2,1,0:T(8,128)(2,1)} async-done(((bf16[8,1,128,1024]{3,2,1,0:T(8,128)(2,1)}), bf16[1,1,128,1024]{3,2,1,0:T(8,128)(2,1)}) %reduce-scatter.23.cloned.1.call-update) | async-done | bytes 262160 | tf_op jit(solution)/shard_map/reduce_scatter | solution.py:299
  1660.8 52.8 %reduce-scatter.21.cloned.1.call-done = bf16[1,1,32,8192]{3,2,1,0:T(8,128)(2,1)} async-done(((bf16[8,1,32,8192]{3,2,1,0:T(8,128)(2,1)}), bf16[1,1,32,8192]{3,2,1,0:T(8,128)(2,1)}) %reduce-scatter.21.cloned.1.call-update) | async-done | bytes 524304 | tf_op jit(solution)/shard_map/reduce_scatter | solution.py:299
  (279 shorter events, 150.0 us)
Async XLA Ops:
  7.2 50.8 %all-gather.5.cloned.1.call-start = ((), (), s32[]{:S(2)}) async-start(), calls=%async_computation.8 | async-start | bytes 7077888 | tf_op jit(solution)/shard_map/all_gather | solution.py:194
  7.9 161.6 %all-gather.7.cloned.1.call-start = ((), (), s32[]{:S(2)}) async-start(), calls=%async_computation.9 | async-start | bytes 2359296 | tf_op jit(solution)/shard_map/all_gather | solution.py:195
  8.7 178.8 %all-gather.9.cloned.1.call-start = ((), (), s32[]{:S(2)}) async-start(), calls=%async_computation.10 | async-start | bytes 18874368 | tf_op jit(solution)/shard_map/all_gather | solution.py:196
  63.5 8.8 copy-start.22
  66.2 53.2 %all-to-all-start = ((bf16[256,3,1024]{0,1,2:T(4,128)(2,1)}), bf16[256,3,1024]{0,1,2:T(4,128)(2,1)S(1)}, u32[]{:S(2)}, u32[]{:S(2)}) async-start(bf16[256,3,1024]{0,1,2:T(4,128)(2,1)} %copy.92), calls=%async_computation | async-start | bytes 4194304 | tf_op jit(solution)/shard_map/all_to_all | solution.py:200
  70.8 164.6 %all-gather.11.cloned.1.call-start = ((), (), s32[]{:S(2)}) async-start(), calls=%async_computation.11 | async-start | bytes 9437184 | tf_op jit(solution)/shard_map/all_gather | solution.py:197
  72.3 61.1 %copy-start.36 = (f32[4,64]{1,0:T(4,128)}, f32[4,64]{1,0:T(4,128)S(1)}, u32[]{:S(2)}) copy-start(f32[4,64]{1,0:T(4,128)S(1)} %mul.496) | copy-start | bytes 3076
  74.2 54.3 %copy-start.23 = (f32[1024,32]{0,1:T(8,128)}, f32[1024,32]{0,1:T(8,128)S(1)}, u32[]{:S(2)}) copy-start(f32[1024,32]{0,1:T(8,128)S(1)} %get-tuple-element.371) | copy-start | bytes 393220
  163.0 23.9 %copy-start.10 = (bf16[1,256,1024]{2,1,0:T(8,128)(2,1)S(1)}, bf16[1,256,1024]{2,1,0:T(8,128)(2,1)}, u32[]{:S(2)}) copy-start(bf16[1,256,1024]{2,1,0:T(8,128)(2,1)} %param.16) | copy-start | bytes 1572868
  163.0 23.9 %copy-start.40 = (f32[1024]{0:T(1024)S(1)}, f32[1024]{0:T(1024)}, u32[]{:S(2)}) copy-start(f32[1024]{0:T(1024)} %param.25) | copy-start | bytes 12292
  165.7 17.6 %all-to-all-start.1 = ((bf16[4,256,256]{1,2,0:T(8,128)(2,1)}), bf16[4,256,256]{1,2,0:T(8,128)(2,1)S(1)}, u32[]{:S(2)}, u32[]{:S(2)}) async-start(bf16[4,256,256]{1,2,0:T(8,128)(2,1)} %copy.100), calls=%async_computation.1 | async-start | bytes 1048576 | tf_op jit(solution)/shard_map/all_to_all | solution.py:213
  187.5 12.3 copy-start.38
  187.5 12.3 copy-start.42
  235.4 7.0 copy-start.12
  245.0 10.1 copy-start.17
  272.4 7.8 copy-start.15
  275.4 19.7 %all-to-all-start.2 = ((bf16[256,4,256]{0,2,1:T(8,128)(2,1)}), bf16[256,4,256]{0,2,1:T(8,128)(2,1)S(1)}, u32[]{:S(2)}, u32[]{:S(2)}) async-start(bf16[256,4,256]{0,2,1:T(8,128)(2,1)} %bitcast.275), calls=%async_computation.2 | async-start | bytes 1048576 | tf_op jit(solution)/shard_map/all_to_all | solution.py:251
  299.0 62.1 %copy-start.33 = (f32[2,512,4]{1,0,2:T(2,128)S(1)}, f32[2,512,4]{1,0,2:T(2,128)}, u32[]{:S(2)}) copy-start(f32[2,512,4]{1,0,2:T(2,128)} %copy-done.32) | copy-start | bytes 49156
  299.0 62.1 %copy-start.37 = (f32[4,64]{1,0:T(4,128)S(1)}, f32[4,64]{1,0:T(4,128)}, u32[]{:S(2)}) copy-start(f32[4,64]{1,0:T(4,128)} %copy-done.36) | copy-start | bytes 3076
  361.1 6.9 copy-start.5
  361.1 6.9 copy-start.7
  361.1 6.9 copy-start.31
  361.1 6.9 copy-start.35
  371.1 7.3 copy-start.14
  373.8 6.7 copy-start.18
  373.8 52.4 %all-to-all-start.3 = ((bf16[1024,3,256]{2,1,0:T(4,128)(2,1)}), bf16[1024,3,256]{2,1,0:T(4,128)(2,1)}, u32[]{:S(2)}, u32[]{:S(2)}) async-start(bf16[1024,3,256]{2,1,0:T(4,128)(2,1)} %copy.107), calls=%async_computation.3 | async-start | bytes 4194304 | tf_op jit(solution)/shard_map/all_to_all | solution.py:265
  378.4 1158.0 %all-reduce.19.cloned.1.call-start = ((), (), s32[]{:S(2)}) async-start(), calls=%async_computation.16 | async-start | bytes 67108864
  434.2 1173.5 %reduce-scatter.19.cloned.1.call-start = ((), (), s32[]{:S(2)}) async-start(), calls=%async_computation.13 | async-start | bytes 589824 | tf_op jit(solution)/shard_map/reduce_scatter | solution.py:299
  1539.0 75.7 %reduce-scatter.17.cloned.1.call-start = ((), (), s32[]{:S(2)}) async-start(), calls=%async_computation.12 | async-start | bytes 1769472 | tf_op jit(solution)/shard_map/reduce_scatter | solution.py:299
  1542.3 116.7 %reduce-scatter.23.cloned.1.call-start = ((), (), s32[]{:S(2)}) async-start(), calls=%async_computation.15 | async-start | bytes 2359296 | tf_op jit(solution)/shard_map/reduce_scatter | solution.py:299
  1546.2 167.4 %reduce-scatter.21.cloned.1.call-start = ((), (), s32[]{:S(2)}) async-start(), calls=%async_computation.14 | async-start | bytes 4718592 | tf_op jit(solution)/shard_map/reduce_scatter | solution.py:299
  1551.9 50.1 %copy-start.16 = (f32[256,1024]{1,0:T(8,128)S(1)}, f32[256,1024]{1,0:T(8,128)}, u32[]{:S(2)}) copy-start(f32[256,1024]{1,0:T(8,128)} %copy-done.15) | copy-start | bytes 3145732
  (34 other events, 94.6 us)
Sparse Core Ops, SparseCore 0:
  9.9 48.1 all-gather.4
  59.9 27.7 all-gather.6
  89.6 89.7 all-gather.8
  181.1 54.2 all-gather.10
  434.4 1102.0 all-reduce.18
  1539.9 33.0 reduce-scatter.18
  1576.3 38.3 reduce-scatter.16
  1617.9 41.0 reduce-scatter.22
  1662.4 51.1 reduce-scatter.20
where the time goes:
time: 1730 us; the launch traced here: 1720 us
  waiting for transfers between devices  1390 us (80%)
  matrix products  116 us (7%)
  local copies, waits for them, and re-layouts  84.5 us (5%)
  other arithmetic  52.8 us (3%)
  blocking collectives  39.2 us (2%)
  starting transfers between devices  18.4 us (1%)
    unnamed x10, waiting for transfers between devices  1100 us
    reduce_scatter x4, waiting for transfers between devices, body(): lax.psum_scatter(as_sent(within), 'dp', scatter_dimension=0, tiled=True)  101 us
    all_gather x1, waiting for transfers between devices, body(): lax.all_gather(w_qkv, 'dp', axis=0, tiled=True)  48.6 us
    all_to_all x1, waiting for transfers between devices, body(): lax.all_to_all(projected.reshape(-1, 3, model_width), 'seq', split_axis=2...  45.2 us
    unnamed x2, blocking collectives  39.2 us
  transfers between devices with their start and end apart: 13, of which 10 were waited for; matrix products, arithmetic and copies ran while one was open for 7% of the time, Pallas kernels for 0%

commit v1 on v0

--- a/solution.py
+++ b/solution.py
@@ -270,35 +270,31 @@
     grad_s_qk = lax.dynamic_update_slice_in_dim(
         jnp.zeros((model_width,), jnp.float32), grad_head_gain.reshape(-1), offset, 0
     )
-    grad_terms = (
-        grad_w_qkv,
-        grad_w_attn_out,
-        grad_w_in,
-        grad_w_down,
-        grad_s_qk,
-        grad_s_u,
-        grad_s_v,
-        grad_alpha_attn,
-        grad_alpha_mlp,
-    )
-    shaped = tuple(
+    big_terms = (grad_w_qkv, grad_w_attn_out, grad_w_in, grad_w_down)
+    across = tuple(
         (
-            term_arr.reshape(
-                (dp_count, seq_count, term_arr.shape[0] // (dp_count * seq_count))
-                + term_arr.shape[1:]
-            )
-            for term_arr in grad_terms
-        )
-    )
-    within = jax.tree.map(
-        lambda part: part.astype(jnp.float32),
-        lax.psum_scatter(as_sent(shaped), "seq", scatter_dimension=1, tiled=True),
-    )
-    across = jax.tree.map(
-        lambda part: part.astype(jnp.float32),
-        lax.psum_scatter(as_sent(within), "dp", scatter_dimension=0, tiled=True),
-    )
-    shards = tuple((term_arr.reshape(term_arr.shape[2:]) for term_arr in across))
+            lax.psum_scatter(term, "dp", scatter_dimension=0, tiled=True)
+            for term in as_sent(big_terms)
+        )
+    )
+    big_shards = tuple(
+        (
+            lax.psum_scatter(term, "seq", scatter_dimension=0, tiled=True).astype(jnp.float32)
+            for term in across
+        )
+    )
+    small_terms = (grad_s_qk, grad_s_u, grad_s_v, grad_alpha_attn, grad_alpha_mlp)
+    packed = jnp.concatenate(
+        [term.reshape(dp_count * seq_count, -1) for term in small_terms], axis=1
+    )
+    packed = lax.psum_scatter(packed, ("dp", "seq"), scatter_dimension=0, tiled=True).reshape(-1)
+    small_shards = []
+    place = 0
+    for term in small_terms:
+        width = term.shape[0] // (dp_count * seq_count)
+        small_shards.append(packed[place : place + width])
+        place += width
+    shards = big_shards + tuple(small_shards)
     return (output, grad_inputs.reshape(tokens.shape)) + tuple(shards)
 
 

time: 1730 us -> 843 us (0.49)
  waiting for transfers between devices: 1390 us -> 459 us
  blocking collectives: 39.2 us -> 90.3 us
    unnamed x10 -> x14, waiting for transfers between devices: 1100 us -> 42 us
    reduce_scatter x4 -> x6, waiting for transfers between devices: 101 us -> 261 us  [the longest x3 195 us: body(): lax.psum_scatter(term, 'dp', scatter_dimension=0, tiled=True)]
    all_to_all x0 -> x1, blocking collectives: none -> 50.3 us  [body(): lax.all_to_all(grad_stack, 'seq', split_axis=0, concat_axis=2, tiled=True)]
    all_to_all x1 -> x0, waiting for transfers between devices: 28 us -> none  [body(): lax.all_to_all(grad_stack, 'seq', split_axis=0, concat_axis=2, tiled=True)]
    unnamed x2 -> x1, blocking collectives: 39.2 us -> 40 us
  transfers between devices with their start and end apart: 13 -> 15, of which waited for: 10 -> 10; matrix products, arithmetic and copies ran while one was open for 7% -> 22% of each run, Pallas kernels for 0% -> 0%
where the time goes in v1:
time: 843 us; the launch traced here: 837 us
  waiting for transfers between devices  459 us (54%)
  matrix products  119 us (14%)
  blocking collectives  90.3 us (11%)
  local copies, waits for them, and re-layouts  86 us (10%)
  other arithmetic  45.4 us (5%)
  between operations  15.3 us (2%)
  starting transfers between devices  13.4 us (2%)
    reduce_scatter x3, waiting for transfers between devices, body(): lax.psum_scatter(term, 'dp', scatter_dimension=0, tiled=True)  195 us
    reduce_scatter x3, waiting for transfers between devices, body(): lax.psum_scatter(term, 'seq', scatter_dimension=0, tiled=True)  66.4 us
    all_to_all x1, blocking collectives, body(): lax.all_to_all(grad_stack, 'seq', split_axis=0, concat_axis=2, tiled=True)  50.3 us
    all_gather x1, waiting for transfers between devices, body(): lax.all_gather(w_qkv, 'dp', axis=0, tiled=True)  48.6 us
    all_to_all x1, waiting for transfers between devices, body(): lax.all_to_all(projected.reshape(-1, 3, model_width), 'seq', split_axis=2...  45.2 us
    unnamed x14, waiting for transfers between devices  42 us
    unnamed x1, blocking collectives  40 us
    all_gather x1, waiting for transfers between devices, body(): lax.all_gather(w_down, 'dp', axis=0, tiled=True)  36.6 us
  transfers between devices with their start and end apart: 15, of which 10 were waited for; matrix products, arithmetic and copies ran while one was open for 22% of the time, Pallas kernels for 0%

profile of v1, /device:TPU:0, one launch (start us, length us, event | category | flops | bytes accessed | tf_op | source)
XLA Modules:
  0.0 836.8 jit_solution(13005143793615328702)
XLA Ops:
  9.4 48.6 %all-gather.5.cloned.1.call-done = bf16[1024,3072]{1,0:T(8,128)(2,1)} async-done(((bf16[128,3072]{1,0:T(8,128)(2,1)}), bf16[1024,3072]{1,0:T(8,128)(2,1)}) %all-gather.5.cloned.1.call-update) | async-done | bytes 6291472 | tf_op jit(solution)/shard_map/all_gather | solution.py:194
  58.0 4.8 convolution_convert_fusion.2
  66.2 4.6 all-to-all-start
  74.2 45.2 %all-to-all-done = bf16[256,3,1024]{0,1,2:T(4,128)(2,1)S(1)} async-done(((bf16[256,3,1024]{0,1,2:T(4,128)(2,1)}), bf16[256,3,1024]{0,1,2:T(4,128)(2,1)S(1)}, u32[]{:S(2)}, u32[]{:S(2)}) %all-to-all-start) | async-done | bytes 1572896 | tf_op jit(solution)/shard_map/all_to_all | solution.py:200
  135.4 23.9 %while.27 = (s32[]{:T(128)}, bf16[2,512,4,64]{1,3,2,0:T(8,128)(2,1)}, f32[2,4,512]{2,1,0:T(4,128)S(1)}, s32[2]{0:T(128)S(1)}, s32[1024]{0:T(1024)S(1)}, /*index=...) while((s32[]{:T(128)}, ...), condition=%wide.region_7.8_spmd, body=%wide.region_4.7_spmd.sunk | while | flops 565312512 | bytes 33111280 | solution.py:116
  162.1 3.7 all-to-all-start.1
  165.9 14.0 %all-to-all-done.1 = bf16[4,256,256]{1,2,0:T(8,128)(2,1)S(1)} async-done(((bf16[4,256,256]{1,2,0:T(8,128)(2,1)}), bf16[4,256,256]{1,2,0:T(8,128)(2,1)S(1)}, u32[]{:S(2)}, u32[]{:S(2)}) %all-to-all-start.1) | async-done | bytes 524320 | tf_op jit(solution)/shard_map/all_to_all | solution.py:213
  183.9 9.4 %fusion.61 = f32[256,8192]{1,0:T(8,128)S(1)} fusion(bf16[1024,8192]{1,0:T(8,128)(2,1)} %all-gather.9.cloned.1.call-done, f32[256,1024]{1,0:T(8,128)S(1)} %get-tuple-element.365, f32[256]{0:T(256)S(1)} %add_rsqrt_fusion.4), kind=kOutput, calls=%fused_computation.164 | convolution fusion | flops 4295491584 | bytes 26215424 | tf_op jit(solution)/shard_map/dot_general | solution.py:218
  198.8 36.6 %all-gather.11.cloned.1.call-done = bf16[4096,1024]{1,0:T(8,128)(2,1)} async-done(((bf16[512,1024]{1,0:T(8,128)(2,1)}), bf16[4096,1024]{1,0:T(8,128)(2,1)}) %all-gather.11.cloned.1.call-update) | async-done | bytes 8388624 | tf_op jit(solution)/shard_map/all_gather | solution.py:197
  235.4 6.4 multiply_reduce_fusion.11
  246.5 8.8 %multiply_reduce_fusion.1 = (f32[4096]{0:T(1024)}, f32[4096]{0:T(1024)}, f32[256,4096]{1,0:T(8,128)S(1)}, bf16[256,4096]{1,0:T(8,128)(2,1)}) fusion(f32[256,8192]{1,0:T(8,128)S(1)} %copy-done.6, f32[4096]{0:T(1024)S(1)} %copy-done.52, f32[4096]{0:T(1024)S(1)} %copy-done.56, bf16[256,1024]{1,0:T(8,128)(2,1)S(1)} %get-tuple-element.383, ...), kind=kOutput, calls=%fused_computation.64 | convolution fusion | flops 2167398400 | bytes 23658496 | tf_op jit(solution)/shard_map/dot_general | solution.py:41
  257.0 19.2 %multiply_reduce_fusion.8 = (f32[256]{0:T(256)S(1)}, f32[256,1024]{1,0:T(8,128)}) fusion(f32[256,1024]{1,0:T(8,128)S(1)} %get-tuple-element.365, f32[256]{0:T(256)S(1)} %add_rsqrt_fusion.4, bf16[1024,8192]{1,0:T(8,128)(2,1)} %all-gather.9.cloned.1.call-done, bf16[256,4096]{1,0:T(8,128)(2,1)} %multiply_convert_fusion.1, ...), kind=kOutput, calls=%fused_computation.101 | convolution fusion | flops 4305977344 | bytes 24649728 | tf_op jit(solution)/shard_map/dot_general | solution.py:41
  282.0 4.6 all-to-all-start.2
  289.8 11.8 %all-to-all-done.2 = bf16[256,4,256]{0,2,1:T(8,128)(2,1)} async-done(((bf16[256,4,256]{0,2,1:T(8,128)(2,1)}), bf16[256,4,256]{0,2,1:T(8,128)(2,1)}, u32[]{:S(2)}, u32[]{:S(2)}) %all-to-all-start.2) | async-done | bytes 524320 | tf_op jit(solution)/shard_map/all_to_all | solution.py:251
  306.2 68.6 %while.28 = (s32[]{:T(128)}, f32[1024,4,64]{0,2,1:T(8,128)S(1)}, f32[1024,4,64]{0,2,1:T(8,128)}, f32[2,512,4,64]{1,0,3,2:T(2,128)}, bf16[2,512,4,64]{1,3,2,0:T(8...) while((s32[]{:T(128)}, f32[1024,4,64]{0,2,1:T(8,128)S(1)}, ...), condition=%wide.region_18.19_spmd.clone, body=%wide.region_16.18_spmd.clone.sunk | while | flops 1378221056 | bytes 166796720 | solution.py:162
  321.5 10.4 %dynamic_update_slice.24 = f32[2,512,4,64]{1,0,3,2:T(2,128)} dynamic-update-slice(f32[2,512,4,64]{1,0,3,2:T(2,128)} %get-tuple-element.603, f32[1,512,4,64]{1,0,3,2:T(1,128)S(1)} %copy.118, s32[]{:T(128)} %get-tuple-element.600, s32[]{:T(128)} %constant.51.clone.1..sunk.1, s32[]{:T(128)} %constant.51.clone.1..sunk.1, s32[]{:T(128)} %constant.51.clone.1..sunk.1) | dynamic-update-slice | bytes 1048580 | tf_op jit(solution)/shard_map/while/body/jit(dynamic_update_index_in_dim)/dynamic_update_slice | solution.py:162
  336.6 3.5 fusion.126
  355.2 10.4 %dynamic_update_slice.24 = f32[2,512,4,64]{1,0,3,2:T(2,128)} dynamic-update-slice(f32[2,512,4,64]{1,0,3,2:T(2,128)} %get-tuple-element.603, f32[1,512,4,64]{1,0,3,2:T(1,128)S(1)} %copy.118, s32[]{:T(128)} %get-tuple-element.600, s32[]{:T(128)} %constant.51.clone.1..sunk.1, s32[]{:T(128)} %constant.51.clone.1..sunk.1, s32[]{:T(128)} %constant.51.clone.1..sunk.1) | dynamic-update-slice | bytes 1048580 | tf_op jit(solution)/shard_map/while/body/jit(dynamic_update_index_in_dim)/dynamic_update_slice | solution.py:162
  365.6 3.3 fusion.125
  370.3 4.5 fusion.126
  387.6 50.3 %all_to_all.68 = bf16[1024,3,256]{2,1,0:T(4,128)(2,1)S(1)} all-to-all(bf16[1024,3,256]{2,1,0:T(4,128)(2,1)S(1)} %copy.88), channel_id=1, replica_groups=mesh['dp'=8,'seq'=4] {'seq'}, dimensions={0} | all-to-all | bytes 3145728 | tf_op jit(solution)/shard_map/all_to_all | solution.py:265
  438.9 5.9 convert_bitcast_fusion
  444.7 8.5 %copy.93 = bf16[1024,3072]{1,0:T(8,128)(2,1)} copy(bf16[1024,3072]{0,1:T(8,128)(2,1)} %convert_bitcast_fusion) | data formatting | bytes 12582912
  454.9 6.2 convolution_convert_fusion.1
  463.6 10.1 %convolution_convert_fusion = bf16[1024,8192]{1,0:T(8,128)(2,1)} fusion(bf16[256,4096]{1,0:T(8,128)(2,1)S(1)} %copy-done.19, bf16[256,4096]{1,0:T(8,128)(2,1)} %get-tuple-element.370, f32[256,1024]{1,0:T(8,128)S(1)} %copy-done.4, f32[256]{0:T(256)S(1)} %add_rsqrt_fusion.4), kind=kOutput, calls=%fused_computation.60 | convolution fusion | flops 4312268800 | bytes 22021120 | tf_op jit(solution)/shard_map/dot_general | solution.py:35
  474.6 38.8 %reduce-scatter.25.cloned.1.call-done = bf16[128,3072]{1,0:T(8,128)(2,1)} async-done(((bf16[1024,3072]{1,0:T(8,128)(2,1)}), bf16[128,3072]{1,0:T(8,128)(2,1)}) %reduce-scatter.25.cloned.1.call-update) | async-done | bytes 786448
  513.4 74.9 %reduce-scatter.21.cloned.1.call-done = bf16[512,1024]{1,0:T(8,128)(2,1)} async-done(((bf16[4096,1024]{1,0:T(8,128)(2,1)}), bf16[512,1024]{1,0:T(8,128)(2,1)}) %reduce-scatter.21.cloned.1.call-update) | async-done | bytes 1048592 | tf_op jit(solution)/shard_map/reduce_scatter | solution.py:276
  588.4 119.7 %reduce-scatter.17.cloned.1.call-done = bf16[128,8192]{1,0:T(8,128)(2,1)} async-done(((bf16[1024,8192]{1,0:T(8,128)(2,1)}), bf16[128,8192]{1,0:T(8,128)(2,1)}) %reduce-scatter.17.cloned.1.call-update) | async-done | bytes 2097168 | tf_op jit(solution)/shard_map/reduce_scatter | solution.py:276
  708.7 40.0 %all-reduce = f32[32,352]{1,0:T(8,128)S(1)} all-reduce(f32[32,352]{1,0:T(8,128)S(1)} %concatenate.46), channel_id=10, replica_groups=mesh['dp'=8,'seq'=4] {'dp','seq'}, use_global_device_ids=true, to_apply=%region_34.35.clone | all-reduce | flops 11264 | bytes 90112
  749.9 5.6 fusion.50
  759.4 23.9 %reduce-scatter.23.cloned.1.call-done = bf16[128,1024]{1,0:T(8,128)(2,1)} async-done(((bf16[512,1024]{1,0:T(8,128)(2,1)}), bf16[128,1024]{1,0:T(8,128)(2,1)}) %reduce-scatter.23.cloned.1.call-update) | async-done | bytes 262160 | tf_op jit(solution)/shard_map/reduce_scatter | solution.py:282
  785.1 42.5 %reduce-scatter.19.cloned.1.call-done = bf16[32,8192]{1,0:T(8,128)(2,1)} async-done(((bf16[128,8192]{1,0:T(8,128)(2,1)}), bf16[32,8192]{1,0:T(8,128)(2,1)}) %reduce-scatter.19.cloned.1.call-update) | async-done | bytes 524304 | tf_op jit(solution)/shard_map/reduce_scatter | solution.py:282
  (299 shorter events, 137.0 us)
Async XLA Ops:
  7.2 50.8 %all-gather.5.cloned.1.call-start = ((), (), s32[]{:S(2)}) async-start(), calls=%async_computation.12 | async-start | bytes 7077888 | tf_op jit(solution)/shard_map/all_gather | solution.py:194
  7.9 157.9 %all-gather.7.cloned.1.call-start = ((), (), s32[]{:S(2)}) async-start(), calls=%async_computation.13 | async-start | bytes 2359296 | tf_op jit(solution)/shard_map/all_gather | solution.py:195
  8.7 175.2 %all-gather.9.cloned.1.call-start = ((), (), s32[]{:S(2)}) async-start(), calls=%async_computation.14 | async-start | bytes 18874368 | tf_op jit(solution)/shard_map/all_gather | solution.py:196
  66.2 53.2 %all-to-all-start = ((bf16[256,3,1024]{0,1,2:T(4,128)(2,1)}), bf16[256,3,1024]{0,1,2:T(4,128)(2,1)S(1)}, u32[]{:S(2)}, u32[]{:S(2)}) async-start(bf16[256,3,1024]{0,1,2:T(4,128)(2,1)} %copy.73), calls=%async_computation | async-start | bytes 4194304 | tf_op jit(solution)/shard_map/all_to_all | solution.py:200
  70.8 164.6 %all-gather.11.cloned.1.call-start = ((), (), s32[]{:S(2)}) async-start(), calls=%async_computation.15 | async-start | bytes 9437184 | tf_op jit(solution)/shard_map/all_gather | solution.py:197
  72.8 59.5 %copy-start.50 = (f32[4,64]{1,0:T(4,128)}, f32[4,64]{1,0:T(4,128)S(1)}, u32[]{:S(2)}) copy-start(f32[4,64]{1,0:T(4,128)S(1)} %mul.496) | copy-start | bytes 3076
  74.2 53.5 %copy-start.38 = (f32[1024,32]{0,1:T(8,128)}, f32[1024,32]{0,1:T(8,128)S(1)}, u32[]{:S(2)}) copy-start(f32[1024,32]{0,1:T(8,128)S(1)} %get-tuple-element.396) | copy-start | bytes 393220
  159.4 24.0 %copy-start.30 = (bf16[1,256,1024]{2,1,0:T(8,128)(2,1)S(1)}, bf16[1,256,1024]{2,1,0:T(8,128)(2,1)}, u32[]{:S(2)}) copy-start(bf16[1,256,1024]{2,1,0:T(8,128)(2,1)} %param.16) | copy-start | bytes 1572868
  159.4 24.0 %copy-start.54 = (f32[1024]{0:T(1024)S(1)}, f32[1024]{0:T(1024)}, u32[]{:S(2)}) copy-start(f32[1024]{0:T(1024)} %param.25) | copy-start | bytes 12292
  162.1 17.7 %all-to-all-start.1 = ((bf16[4,256,256]{1,2,0:T(8,128)(2,1)}), bf16[4,256,256]{1,2,0:T(8,128)(2,1)S(1)}, u32[]{:S(2)}, u32[]{:S(2)}) async-start(bf16[4,256,256]{1,2,0:T(8,128)(2,1)} %copy.81), calls=%async_computation.1 | async-start | bytes 1048576 | tf_op jit(solution)/shard_map/all_to_all | solution.py:213
  183.9 92.3 %copy-start.3 = (f32[256,1024]{1,0:T(8,128)}, f32[256,1024]{1,0:T(8,128)S(1)}, u32[]{:S(2)}) copy-start(f32[256,1024]{1,0:T(8,128)S(1)} %get-tuple-element.365) | copy-start | bytes 3145732
  183.9 12.6 %copy-start.52 = (f32[4096]{0:T(1024)S(1)}, f32[4096]{0:T(1024)}, u32[]{:S(2)}) copy-start(f32[4096]{0:T(1024)} %param.24) | copy-start | bytes 49156
  183.9 12.6 %copy-start.56 = (f32[4096]{0:T(1024)S(1)}, f32[4096]{0:T(1024)}, u32[]{:S(2)}) copy-start(f32[4096]{0:T(1024)} %param.23) | copy-start | bytes 49156
  198.8 43.5 %copy-start.26 = (bf16[1,256,1024]{2,1,0:T(8,128)(2,1)S(1)}, bf16[1,256,1024]{2,1,0:T(8,128)(2,1)}, u32[]{:S(2)}) copy-start(bf16[1,256,1024]{2,1,0:T(8,128)(2,1)} %param.27) | copy-start | bytes 1572868
  282.0 19.6 %all-to-all-start.2 = ((bf16[256,4,256]{0,2,1:T(8,128)(2,1)}), bf16[256,4,256]{0,2,1:T(8,128)(2,1)}, u32[]{:S(2)}, u32[]{:S(2)}) async-start(bf16[256,4,256]{0,2,1:T(8,128)(2,1)} %bitcast.22), calls=%async_computation.2 | async-start | bytes 1048576 | tf_op jit(solution)/shard_map/all_to_all | solution.py:251
  286.6 187.2 %reduce-scatter.13.cloned.1.call-start = ((), (), s32[]{:S(2)}) async-start(), calls=%async_computation.16 | async-start | bytes 2359296 | tf_op jit(solution)/shard_map/reduce_scatter | solution.py:276
  289.8 223.6 %reduce-scatter.25.cloned.1.call-start = ((), (), s32[]{:S(2)}) async-start(), calls=%async_computation.22 | async-start | bytes 7077888
  306.2 68.7 %copy-start.47 = (f32[2,512,4]{1,0,2:T(2,128)S(1)}, f32[2,512,4]{1,0,2:T(2,128)}, u32[]{:S(2)}) copy-start(f32[2,512,4]{1,0,2:T(2,128)} %copy-done.46) | copy-start | bytes 49156
  306.2 68.7 %copy-start.51 = (f32[4,64]{1,0:T(4,128)S(1)}, f32[4,64]{1,0:T(4,128)}, u32[]{:S(2)}) copy-start(f32[4,64]{1,0:T(4,128)} %copy-done.50) | copy-start | bytes 3076
  453.3 135.0 %reduce-scatter.21.cloned.1.call-start = ((), (), s32[]{:S(2)}) async-start(), calls=%async_computation.20 | async-start | bytes 9437184 | tf_op jit(solution)/shard_map/reduce_scatter | solution.py:276
  461.2 246.9 %reduce-scatter.17.cloned.1.call-start = ((), (), s32[]{:S(2)}) async-start(), calls=%async_computation.18 | async-start | bytes 18874368 | tf_op jit(solution)/shard_map/reduce_scatter | solution.py:276
  473.7 234.4 %copy-start.55 = (f32[1024]{0:T(1024)S(1)}, f32[1024]{0:T(1024)}, u32[]{:S(2)}) copy-start(f32[1024]{0:T(1024)} %param.25) | copy-start | bytes 12292
  473.7 234.4 %copy-start.60 = (f32[1024]{0:T(1024)S(1)}, f32[1024]{0:T(1024)}, u32[]{:S(2)}) copy-start(f32[1024]{0:T(1024)} %get-tuple-element.312) | copy-start | bytes 12292
  473.7 234.5 %copy-start.57 = (f32[1024]{0:T(1024)S(1)}, f32[1024]{0:T(1024)}, u32[]{:S(2)}) copy-start(f32[1024]{0:T(1024)} %get-tuple-element.308) | copy-start | bytes 12292
  473.7 234.9 %copy-start.58 = (f32[4096]{0:T(1024)S(1)}, f32[4096]{0:T(1024)}, u32[]{:S(2)}) copy-start(f32[4096]{0:T(1024)} %get-tuple-element.306) | copy-start | bytes 49156
  473.7 234.9 %copy-start.59 = (f32[4096]{0:T(1024)S(1)}, f32[4096]{0:T(1024)}, u32[]{:S(2)}) copy-start(f32[4096]{0:T(1024)} %get-tuple-element.307) | copy-start | bytes 49156
  473.8 276.2 %copy-start.18 = (bf16[256,3,4,256]{0,3,2,1:T(8,128)(2,1)S(1)}, bf16[256,3,4,256]{0,3,2,1:T(8,128)(2,1)}, u32[]{:S(2)}) copy-start(bf16[256,3,4,256]{0,3,2,1:T(8,128)(2,1)} %copy-done.17) | copy-start | bytes 4718596
  473.8 276.2 %copy-start.32 = (f32[256,1024]{1,0:T(8,128)S(1)}, f32[256,1024]{1,0:T(8,128)}, u32[]{:S(2)}) copy-start(f32[256,1024]{1,0:T(8,128)} %copy-done.31) | copy-start | bytes 3145732
  473.8 281.8 %reduce-scatter.15.cloned.1.call-start = ((), (), s32[]{:S(2)}) async-start(), calls=%async_computation.17 | async-start | bytes 327680 | tf_op jit(solution)/shard_map/reduce_scatter | solution.py:282
  474.5 282.6 %reduce-scatter.27.cloned.1.call-start = ((), (), s32[]{:S(2)}) async-start(), calls=%async_computation.23 | async-start | bytes 983040
  513.3 269.9 %reduce-scatter.23.cloned.1.call-start = ((), (), s32[]{:S(2)}) async-start(), calls=%async_computation.21 | async-start | bytes 1310720 | tf_op jit(solution)/shard_map/reduce_scatter | solution.py:282
  588.3 239.3 %reduce-scatter.19.cloned.1.call-start = ((), (), s32[]{:S(2)}) async-start(), calls=%async_computation.19 | async-start | bytes 2621440 | tf_op jit(solution)/shard_map/reduce_scatter | solution.py:282
  (53 other events, 200.4 us)
Sparse Core Ops, SparseCore 0:
  9.9 48.1 all-gather.4
  59.9 27.8 all-gather.6
  89.6 89.7 all-gather.8
  181.1 54.2 all-gather.10
  290.4 41.6 reduce-scatter.12
  453.4 59.8 reduce-scatter.24
  516.8 71.4 reduce-scatter.20
  591.9 116.1 reduce-scatter.16
  710.4 20.0 reduce-scatter.14
  732.6 21.5 reduce-scatter.26
  756.5 26.7 reduce-scatter.22
  785.4 42.1 reduce-scatter.18

commit v2 on v1

--- a/solution.py
+++ b/solution.py
@@ -1,9 +1,15 @@
+import functools
 import math
 
 import jax
 import jax.numpy as jnp
 from jax import lax
+from jax.experimental import pallas as pl
+from jax.experimental.pallas import tpu as pltpu
 from jax.sharding import PartitionSpec as P
+
+MESH_ID = pl.DeviceIdType.MESH
+TEAM = 4
 
 HEADS = 16
 HD = 64
@@ -12,14 +18,6 @@
 EPS = 1e-06
 ROPE_BASE = 10000.0
 MASKED_SCORE = -1e30
-
-
-def as_sent(array):
-
-    def short(part):
-        return part.astype(jnp.bfloat16) if part.dtype == jnp.float32 else part
-
-    return jax.tree.map(short, array)
 
 
 def rms_norm(values):
@@ -163,6 +161,212 @@
         one_block, (zeros_init, zeros_init), (query_blocks, grad_blocks, log_sums, starts)
     )
     return (grad_query.reshape(length, groups, head_dim), grad_key, grad_value)
+
+
+def greet(peers):
+    barrier = pltpu.get_barrier_semaphore()
+    for peer in peers:
+        pl.semaphore_signal(barrier, inc=1, device_id=peer, device_id_type=MESH_ID)
+    pl.semaphore_wait(barrier, len(peers))
+
+
+def flip(place, bit):
+    return place + bit - 2 * bit * lax.rem(place // bit, 2)
+
+
+def seq_gather_kernel(count, own_ref, out_ref, send_sem, recv_sem, local_sem):
+    rows = own_ref.shape[0]
+    mine = lax.axis_index("seq")
+    peers = [lax.rem(mine + step, count) for step in range(1, count)]
+    greet([{"seq": peer} for peer in peers])
+    spot = pl.ds(pl.multiple_of(mine * rows, rows), rows)
+    copies = []
+    for slot, peer in enumerate(peers):
+        copies.append(
+            pltpu.make_async_remote_copy(
+                src_ref=own_ref,
+                dst_ref=out_ref.at[spot],
+                send_sem=send_sem.at[slot],
+                recv_sem=recv_sem.at[slot],
+                device_id={"seq": peer},
+                device_id_type=MESH_ID,
+            )
+        )
+    for copy in copies:
+        copy.start()
+    local = pltpu.make_async_copy(own_ref, out_ref.at[spot], local_sem)
+    local.start()
+    local.wait()
+    for copy in copies:
+        copy.wait()
+
+
+def seq_gather(own):
+    count = lax.axis_size("seq")
+    rows, width = own.shape
+    return pl.pallas_call(
+        functools.partial(seq_gather_kernel, count),
+        out_shape=jax.ShapeDtypeStruct((count * rows, width), own.dtype),
+        in_specs=[pl.BlockSpec(memory_space=pl.ANY)],
+        out_specs=pl.BlockSpec(memory_space=pl.ANY),
+        scratch_shapes=[
+            pltpu.SemaphoreType.DMA((count - 1,)),
+            pltpu.SemaphoreType.DMA((count - 1,)),
+            pltpu.SemaphoreType.DMA,
+        ],
+        cost_estimate=pl.CostEstimate(
+            flops=0, bytes_accessed=100 * count * rows * width, transcendentals=0
+        ),
+        compiler_params=pltpu.CompilerParams(collective_id=0, has_side_effects=True),
+    )(own)
+
+
+PIECES = 4
+
+
+def team_gather_kernel(own_ref, out_ref, send_sem, recv_sem, local_sem):
+    rows = own_ref.shape[0]
+    piece = rows // PIECES
+    place = lax.axis_index("dp")
+    far, near = flip(place, 2), flip(place, 1)
+    rank, far_rank = lax.rem(place, TEAM), lax.rem(far, TEAM)
+    greet([{"dp": far}, {"dp": near}])
+
+    def spot(owner, index):
+        return out_ref.at[pl.ds(pl.multiple_of(owner * rows + index * piece, piece), piece)]
+
+    def push(source, owner, index, kind, peer):
+        return pltpu.make_async_remote_copy(
+            src_ref=source,
+            dst_ref=spot(owner, index),
+            send_sem=send_sem.at[kind, index],
+            recv_sem=recv_sem.at[kind, index],
+            device_id={"dp": peer},
+            device_id_type=MESH_ID,
+        )
+
+    across = [push(own_ref.at[pl.ds(i * piece, piece)], rank, i, 0, far) for i in range(PIECES)]
+    beside = [push(own_ref.at[pl.ds(i * piece, piece)], rank, i, 1, near) for i in range(PIECES)]
+    for copy in across:
+        copy.start()
+    for copy in beside:
+        copy.start()
+    local = pltpu.make_async_copy(
+        own_ref, out_ref.at[pl.ds(pl.multiple_of(rank * rows, rows), rows)], local_sem
+    )
+    local.start()
+    passed = [push(spot(far_rank, i), far_rank, i, 2, near) for i in range(PIECES)]
+    for i in range(PIECES):
+        across[i].wait_recv()
+        passed[i].start()
+    local.wait()
+    for copy in across:
+        copy.wait_send()
+    for copy in beside:
+        copy.wait()
+    for copy in passed:
+        copy.wait()
+
+
+def team_gather(own):
+    rows, width = own.shape
+    return pl.pallas_call(
+        team_gather_kernel,
+        out_shape=jax.ShapeDtypeStruct((TEAM * rows, width), own.dtype),
+        in_specs=[pl.BlockSpec(memory_space=pl.ANY)],
+        out_specs=pl.BlockSpec(memory_space=pl.ANY),
+        scratch_shapes=[
+            pltpu.SemaphoreType.DMA((3, PIECES)),
+            pltpu.SemaphoreType.DMA((3, PIECES)),
+            pltpu.SemaphoreType.DMA,
+        ],
+        cost_estimate=pl.CostEstimate(
+            flops=0, bytes_accessed=50 * TEAM * rows * width, transcendentals=0
+        ),
+        compiler_params=pltpu.CompilerParams(collective_id=1, has_side_effects=True),
+    )(own)
+
+
+def team_sum_kernel(part_ref, out_ref, near_buf, send_buf, far_buf, send_sem, recv_sem, far_send, far_recv):
+    rows = out_ref.shape[0]
+    piece = rows // PIECES
+    place = lax.axis_index("dp")
+    far, near = flip(place, 2), flip(place, 1)
+    rank, far_rank = lax.rem(place, TEAM), lax.rem(far, TEAM)
+    near_rank = lax.rem(near, TEAM)
+    cross_rank = lax.rem(flip(near, 2), TEAM)
+    greet([{"dp": far}, {"dp": near}])
+
+    def to_near(owner, slot, index):
+        return pltpu.make_async_remote_copy(
+            src_ref=part_ref.at[owner, pl.ds(index * piece, piece)],
+            dst_ref=near_buf.at[slot, pl.ds(index * piece, piece)],
+            send_sem=send_sem.at[slot, index],
+            recv_sem=recv_sem.at[slot, index],
+            device_id={"dp": near},
+            device_id_type=MESH_ID,
+        )
+
+    outward = [to_near(cross_rank, 0, i) for i in range(PIECES)]
+    inward = [to_near(near_rank, 1, i) for i in range(PIECES)]
+    for copy in outward + inward:
+        copy.start()
+    ships = []
+    for i in range(PIECES):
+        here = pl.ds(i * piece, piece)
+        outward[i].wait_recv()
+        send_buf[here] = (
+            part_ref[far_rank, here].astype(jnp.float32) + near_buf[0, here].astype(jnp.float32)
+        ).astype(send_buf.dtype)
+        ships.append(
+            pltpu.make_async_remote_copy(
+                src_ref=send_buf.at[here],
+                dst_ref=far_buf.at[here],
+                send_sem=far_send.at[i],
+                recv_sem=far_recv.at[i],
+                device_id={"dp": far},
+                device_id_type=MESH_ID,
+            )
+        )
+        if i > 0:
+            ships[i - 1].start()
+    for i in range(PIECES):
+        here = pl.ds(i * piece, piece)
+        inward[i].wait_recv()
+        out_ref[here] = part_ref[rank, here].astype(jnp.float32) + near_buf[1, here].astype(
+            jnp.float32
+        )
+        if i == 0:
+            ships[PIECES - 1].start()
+    for i in range(PIECES):
+        here = pl.ds(i * piece, piece)
+        ships[i].wait_recv()
+        out_ref[here] = out_ref[here] + far_buf[here].astype(jnp.float32)
+    for copy in outward + inward + ships:
+        copy.wait_send()
+
+
+def team_sum(part):
+    _, rows, width = part.shape
+    return pl.pallas_call(
+        team_sum_kernel,
+        out_shape=jax.ShapeDtypeStruct((rows, width), jnp.float32),
+        in_specs=[pl.BlockSpec(memory_space=pltpu.VMEM)],
+        out_specs=pl.BlockSpec(memory_space=pltpu.VMEM),
+        scratch_shapes=[
+            pltpu.VMEM((2, rows, width), part.dtype),
+            pltpu.VMEM((rows, width), part.dtype),
+            pltpu.VMEM((rows, width), part.dtype),
+            pltpu.SemaphoreType.DMA((2, PIECES)),
+            pltpu.SemaphoreType.DMA((2, PIECES)),
+            pltpu.SemaphoreType.DMA((PIECES,)),
+            pltpu.SemaphoreType.DMA((PIECES,)),
+        ],
+        cost_estimate=pl.CostEstimate(
+            flops=0, bytes_accessed=50 * TEAM * rows * width, transcendentals=0
+        ),
+        compiler_params=pltpu.CompilerParams(collective_id=2, has_side_effects=True),
+    )(part)
 
 
 def body(
@@ -183,24 +387,53 @@
     inputs_b = tokens.reshape(-1, model_width)
     inputs_f = inputs_b.astype(jnp.float32)
     seg_row = segments.reshape(-1)
+    length = seg_row.shape[0]
+    local_rows = inputs_b.shape[0]
     seq_count = lax.axis_size("seq")
     dp_count = lax.axis_size("dp")
     head_group = HEADS // seq_count
     group_width = head_group * HD
-    offset = lax.axis_index("seq") * group_width
+    seq_rank = lax.axis_index("seq")
+    team_rank = lax.rem(lax.axis_index("dp"), TEAM)
+    offset = seq_rank * group_width
     head_gain = lax.dynamic_slice_in_dim(s_qk, offset, group_width).reshape(head_group, HD)
     score_scale = 1.0 / math.sqrt(HD)
-    full_qkv, full_out, full_in, full_down = (
-        lax.all_gather(w_qkv, "dp", axis=0, tiled=True),
-        lax.all_gather(w_attn_out, "dp", axis=0, tiled=True),
-        lax.all_gather(w_in, "dp", axis=0, tiled=True),
-        lax.all_gather(w_down, "dp", axis=0, tiled=True),
-    )
-    projected = jnp.dot(inputs_b, full_qkv, preferred_element_type=jnp.float32).astype(jnp.bfloat16)
-    by_heads = lax.all_to_all(
-        projected.reshape(-1, 3, model_width), "seq", split_axis=2, concat_axis=0, tiled=True
-    )
-    length = by_heads.shape[0]
+    ff_width = s_u.shape[0]
+    ff_part = ff_width // dp_count // TEAM
+    ff_team = ff_width // TEAM
+    in_rows = w_in.shape[0]
+
+    head_cols = lax.dynamic_slice_in_dim(
+        w_qkv.reshape(-1, 3, model_width), offset, group_width, axis=2
+    ).reshape(-1, 3 * group_width)
+    heads_qkv = lax.all_gather(head_cols, "dp", axis=0, tiled=True)
+    full_out = lax.all_gather(w_attn_out, "dp", axis=0, tiled=True)
+    in_parts = w_in.reshape(in_rows, 2 * dp_count, TEAM, ff_part).transpose(2, 0, 1, 3)
+    ff_blocks = jnp.concatenate(
+        [
+            in_parts.reshape(TEAM, in_rows, 2 * ff_team),
+            w_down.reshape(TEAM, ff_part, model_width),
+        ],
+        axis=2,
+    )
+    ff_blocks = jnp.concatenate([ff_blocks] * (dp_count // TEAM), axis=0)
+    team_ff = lax.all_to_all(ff_blocks, "dp", 0, 0, tiled=True)
+    team_in = team_ff[:, :, : 2 * ff_team].reshape(model_width, 2 * ff_team)
+    team_down = team_ff[:, :, 2 * ff_team :].reshape(ff_team, model_width)
+
+    def team_slice(scale):
+        return lax.dynamic_index_in_dim(
+            scale.reshape(dp_count, TEAM, ff_part), team_rank, 1, keepdims=False
+        ).reshape(ff_team)
+
+    s_u_team, s_v_team = team_slice(s_u), team_slice(s_v)
+
+    seq_tokens = seq_gather(inputs_b)
+    by_heads = (
+        jnp.dot(seq_tokens, heads_qkv, preferred_element_type=jnp.float32)
+        .astype(jnp.bfloat16)
+        .reshape(length, 3, group_width)
+    )
     cosine, sine_tab = rope_tables(doc_positions(seg_row), HD)
     query_unit, query_inv, query_n = head_prep(
         by_heads[:, 0].reshape(length, head_group, HD), cosine, sine_tab, head_gain
@@ -215,16 +448,18 @@
     attn_unit, attn_inv = rms_norm(attn_proj)
     hidden, hidden_inv = rms_norm(inputs_f + alpha_attn * (attn_unit - inputs_f))
     hidden_b = hidden.astype(jnp.bfloat16)
-    up_gate = jnp.dot(hidden_b, full_in, preferred_element_type=jnp.float32)
-    ff_width = s_u.shape[0]
-    up_raw = up_gate[:, :ff_width]
-    gate_raw = up_gate[:, ff_width:]
-    up_val = s_u * up_raw
-    gate_val = s_v * gate_raw
+
+    team_hidden = team_gather(hidden_b)
+    up_gate = jnp.dot(team_hidden, team_in, preferred_element_type=jnp.float32)
+    up_raw = up_gate[:, :ff_team]
+    gate_raw = up_gate[:, ff_team:]
+    up_val = s_u_team * up_raw
+    gate_val = s_v_team * gate_raw
     gate_sig = jax.nn.sigmoid(gate_val)
     silu_gate = gate_val * gate_sig
     inner_act = (silu_gate * up_val).astype(jnp.bfloat16)
-    down_proj = jnp.dot(inner_act, full_down, preferred_element_type=jnp.float32)
+    down_part = jnp.dot(inner_act, team_down, preferred_element_type=jnp.float32)
+    down_proj = team_sum(down_part.astype(jnp.bfloat16).reshape(TEAM, local_rows, model_width))
     mlp_unit, mlp_inv = rms_norm(down_proj)
     result, result_inv = rms_norm(hidden + alpha_mlp * (mlp_unit - hidden))
     output = result.astype(jnp.bfloat16).reshape(tokens.shape)
@@ -232,22 +467,54 @@
     grad_two = rms_back(grad_res, result, result_inv)
     grad_alpha_mlp = jnp.sum(grad_two * (mlp_unit - hidden), axis=0)
     grad_down_proj = rms_back(alpha_mlp * grad_two, mlp_unit, mlp_inv).astype(jnp.bfloat16)
-    grad_w_down = contract_rows(inner_act, grad_down_proj)
-    grad_inner = contract_cols(grad_down_proj, full_down)
+
+    team_grad = team_gather(grad_down_proj)
+    grad_inner = contract_cols(team_grad, team_down)
     grad_up_val = grad_inner * silu_gate
     grad_gate_val = grad_inner * up_val * gate_sig * (1.0 + gate_val * (1.0 - gate_sig))
     grad_s_u = jnp.sum(grad_up_val * up_raw, axis=0)
     grad_s_v = jnp.sum(grad_gate_val * gate_raw, axis=0)
-    grad_up_gate = jnp.concatenate([grad_up_val * s_u, grad_gate_val * s_v], axis=1).astype(
-        jnp.bfloat16
-    )
-    grad_w_in = contract_rows(hidden_b, grad_up_gate)
-    grad_hidden = (1.0 - alpha_mlp) * grad_two + contract_cols(grad_up_gate, full_in)
+    grad_up_gate = jnp.concatenate(
+        [grad_up_val * s_u_team, grad_gate_val * s_v_team], axis=1
+    ).astype(jnp.bfloat16)
+    hidden_part = contract_cols(grad_up_gate, team_in)
+    hidden_sum = team_sum(hidden_part.astype(jnp.bfloat16).reshape(TEAM, local_rows, model_width))
+    grad_hidden = (1.0 - alpha_mlp) * grad_two + hidden_sum
+    grad_w_ff = jnp.concatenate(
+        [contract_rows(team_hidden, grad_up_gate), contract_rows(inner_act, team_grad)], axis=1
+    ).astype(jnp.bfloat16)
+    ff_terms = lax.all_to_all(
+        grad_w_ff.reshape(dp_count, in_rows, 2 * ff_team + model_width), "dp", 0, 0, tiled=True
+    )
+    ff_sums = jnp.sum(
+        ff_terms.reshape(dp_count // TEAM, TEAM, in_rows, -1).astype(jnp.float32), axis=0
+    ).astype(jnp.bfloat16)
+    in_sums = ff_sums[:, :, : 2 * ff_team].transpose(1, 0, 2).reshape(in_rows, 2 * ff_width)
+    shard_w_in = lax.psum_scatter(in_sums, "seq", scatter_dimension=0, tiled=True)
+    shard_w_in = (
+        shard_w_in.reshape(-1, TEAM, 2 * dp_count, ff_part)
+        .transpose(0, 2, 1, 3)
+        .reshape(-1, 2 * ff_width)
+        .astype(jnp.float32)
+    )
+    shard_w_down = lax.psum_scatter(
+        ff_sums[:, :, 2 * ff_team :].reshape(TEAM * ff_part, model_width),
+        "seq",
+        scatter_dimension=0,
+        tiled=True,
+    ).astype(jnp.float32)
+
     grad_one = rms_back(grad_hidden, hidden, hidden_inv)
     grad_alpha_attn = jnp.sum(grad_one * (attn_unit - inputs_f), axis=0)
     grad_attn_proj = rms_back(alpha_attn * grad_one, attn_unit, attn_inv).astype(jnp.bfloat16)
-    grad_w_attn_out = contract_rows(attn_pieces, grad_attn_proj)
     grad_pieces = contract_cols(grad_attn_proj, full_out).astype(jnp.bfloat16)
+    grad_w_attn_out = contract_rows(attn_pieces, grad_attn_proj).astype(jnp.bfloat16)
+    shard_w_attn_out = lax.psum_scatter(
+        lax.psum_scatter(grad_w_attn_out, "dp", scatter_dimension=0, tiled=True),
+        "seq",
+        scatter_dimension=0,
+        tiled=True,
+    ).astype(jnp.float32)
     grad_heads = lax.all_to_all(
         grad_pieces, "seq", split_axis=1, concat_axis=0, tiled=True
     ).reshape(length, head_group, HD)
@@ -257,45 +524,64 @@
     grad_head_gain = jnp.sum(grad_query_n * query_unit + grad_key_n * key_unit, axis=0)
     grad_query = head_back(grad_query_n, query_unit, query_inv, head_gain, cosine, sine_tab)
     grad_key = head_back(grad_key_n, key_unit, key_inv, head_gain, cosine, sine_tab)
-    grad_stack = (
+    grad_qkv = (
         jnp.stack([grad_query, grad_key, grad_value], axis=1)
-        .reshape(length, 3, group_width)
+        .reshape(length, 3 * group_width)
         .astype(jnp.bfloat16)
     )
-    grad_qkv = lax.all_to_all(grad_stack, "seq", split_axis=0, concat_axis=2, tiled=True).reshape(
-        -1, 3 * model_width
-    )
-    grad_w_qkv = contract_rows(inputs_b, grad_qkv)
-    grad_inputs = (1.0 - alpha_attn) * grad_one + contract_cols(grad_qkv, full_qkv)
+    grad_w_qkv = contract_rows(seq_tokens, grad_qkv).astype(jnp.bfloat16)
+    rows_w_qkv = lax.psum_scatter(grad_w_qkv, "dp", scatter_dimension=0, tiled=True)
+    shard_w_qkv = lax.all_to_all(
+        rows_w_qkv.reshape(seq_count, -1, 3 * group_width), "seq", 0, 0, tiled=True
+    )
+    shard_w_qkv = (
+        shard_w_qkv.reshape(seq_count, -1, 3, group_width)
+        .transpose(1, 2, 0, 3)
+        .reshape(-1, 3 * model_width)
+        .astype(jnp.float32)
+    )
+    tokens_part = contract_cols(grad_qkv, heads_qkv).astype(jnp.bfloat16)
+    tokens_terms = lax.all_to_all(
+        tokens_part.reshape(seq_count, local_rows, model_width), "seq", 0, 0, tiled=True
+    )
+    grad_inputs = (1.0 - alpha_attn) * grad_one + jnp.sum(
+        tokens_terms.astype(jnp.float32), axis=0
+    )
+
+    def team_spread(part):
+        whole = jnp.zeros((dp_count, TEAM, ff_part), jnp.float32)
+        return lax.dynamic_update_slice_in_dim(
+            whole, part.reshape(dp_count, 1, ff_part), team_rank, 1
+        ).reshape(ff_width)
+
     grad_s_qk = lax.dynamic_update_slice_in_dim(
         jnp.zeros((model_width,), jnp.float32), grad_head_gain.reshape(-1), offset, 0
     )
-    big_terms = (grad_w_qkv, grad_w_attn_out, grad_w_in, grad_w_down)
-    across = tuple(
-        (
-            lax.psum_scatter(term, "dp", scatter_dimension=0, tiled=True)
-            for term in as_sent(big_terms)
-        )
-    )
-    big_shards = tuple(
-        (
-            lax.psum_scatter(term, "seq", scatter_dimension=0, tiled=True).astype(jnp.float32)
-            for term in across
-        )
-    )
-    small_terms = (grad_s_qk, grad_s_u, grad_s_v, grad_alpha_attn, grad_alpha_mlp)
+    small_terms = (
+        grad_s_qk,
+        team_spread(grad_s_u),
+        team_spread(grad_s_v),
+        grad_alpha_attn,
+        grad_alpha_mlp,
+    )
     packed = jnp.concatenate(
         [term.reshape(dp_count * seq_count, -1) for term in small_terms], axis=1
     )
     packed = lax.psum_scatter(packed, ("dp", "seq"), scatter_dimension=0, tiled=True).reshape(-1)
     small_shards = []
-    place = 0
+    spot = 0
     for term in small_terms:
         width = term.shape[0] // (dp_count * seq_count)
-        small_shards.append(packed[place : place + width])
-        place += width
-    shards = big_shards + tuple(small_shards)
-    return (output, grad_inputs.reshape(tokens.shape)) + tuple(shards)
+        small_shards.append(packed[spot : spot + width])
+        spot += width
+    return (
+        output,
+        grad_inputs.reshape(tokens.shape),
+        shard_w_qkv,
+        shard_w_attn_out,
+        shard_w_in,
+        shard_w_down,
+    ) + tuple(small_shards)
 
 
 def solution(mesh):

time: 843 us -> 646 us (0.77)
  waiting for transfers between devices: 459 us -> 94.2 us
  Pallas kernels: 0 us -> 128 us
  other arithmetic: 45.4 us -> 82.3 us
  matrix products: 119 us -> 87.6 us
  starting transfers between devices: 13.4 us -> 39.2 us
  local copies, waits for them, and re-layouts: 86 us -> 96.5 us
    reduce_scatter x6 -> x5, waiting for transfers between devices: 261 us -> 29 us  [the longest x1 17.9 us: body(): lax.psum_scatter(grad_w_qkv, 'dp', scatter_dimension=0, tiled=True)]
    pallas_call x0 -> x5, Pallas kernels: none -> 128 us  [the longest x2 50.3 us: team_gather(): pl.pallas_call(team_gather_kernel, out_shape=jax.ShapeDtypeStruct((TEAM *...]
    all_to_all x1 -> x0, blocking collectives: 50.3 us -> none  [body(): lax.all_to_all(grad_stack, 'seq', split_axis=0, concat_axis=2, tiled=True)]
    unnamed x1, blocking collectives: 40 us -> 84.1 us
    unnamed x14 -> x7, waiting for transfers between devices: 42 us -> 1.98 us
    all_to_all x1 -> x4, waiting for transfers between devices: 45.2 us -> 5.59 us  [the longest x1 4.08 us: body(): lax.all_to_all(rows_w_qkv.reshape(seq_count, -1, 3 * group_width), 'seq',...]
    all_gather x4 -> x2, waiting for transfers between devices: 85.3 us -> 51.8 us  [the longest x1 51.8 us: body(): full_out = lax.all_gather(w_attn_out, 'dp', axis=0, tiled=True)]
    concatenate x2, other arithmetic: 0.07 us -> 23.5 us  [the longest x1 20.3 us: body(): ff_blocks = jnp.concatenate([ff_blocks] * (dp_count // TEAM), axis=0)]
  transfers between devices with their start and end apart: 15 -> 13, of which waited for: 10 -> 6; matrix products, arithmetic and copies ran while one was open for 22% -> 23% of each run, Pallas kernels for 0% -> 11%
where the time goes in v2:
time: 646 us; the launch traced here: 635 us
  Pallas kernels  128 us (20%)
  local copies, waits for them, and re-layouts  96.5 us (15%)
  waiting for transfers between devices  94.2 us (15%)
  matrix products  87.6 us (14%)
  blocking collectives  84.1 us (13%)
  other arithmetic  82.3 us (13%)
  starting transfers between devices  39.2 us (6%)
  between operations  15.7 us (2%)
  loops' own time  8.09 us (1%)
    unnamed x1, blocking collectives  84.1 us
    all_gather x1, waiting for transfers between devices, body(): full_out = lax.all_gather(w_attn_out, 'dp', axis=0, tiled=True)  51.8 us
    pallas_call x2, Pallas kernels, team_gather(): pl.pallas_call(team_gather_kernel, out_shape=jax.ShapeDtypeStruct((TEAM *...  50.3 us
    pallas_call x1, Pallas kernels, seq_gather(): pl.pallas_call(functools.partial(seq_gather_kernel, count), out_shape=jax...  40.2 us
    pallas_call x2, Pallas kernels, team_sum(): pl.pallas_call(team_sum_kernel, out_shape=jax.ShapeDtypeStruct((rows, wid...  37 us
    dot_general x4, matrix products, contract_cols(): lax.dot_general(left_arr, right_arr, (((1,), (1,)), ((), ())), preferred_...  22.3 us
    dynamic_update_slice x4, local copies, waits for them, and re-layouts, attend_backward(): lax.scan(one_block, (zeros_init, zeros_init), (query_blocks, grad_blocks,...  21.8 us
    unnamed x109, local copies, waits for them, and re-layouts  21.3 us
  transfers between devices with their start and end apart: 13, of which 6 were waited for; matrix products, arithmetic and copies ran while one was open for 23% of the time, Pallas kernels for 11%

profile of v2, /device:TPU:0, one launch (start us, length us, event | category | flops | bytes accessed | tf_op | source)
XLA Modules:
  0.0 635.2 jit_solution(8742355362240475817)
XLA Ops:
  11.7 40.2 %shard_map.203 = bf16[1024,1024]{1,0:T(8,128)(2,1)} custom-call(bf16[256,1024]{1,0:T(8,128)(2,1)} %bitcast.240), custom_call_target="tpu_custom_call" | custom-call | bytes 104857600 | tf_op jit(solution)/shard_map/pallas_call | solution.py:207
  62.9 23.9 %while.27 = (s32[]{:T(128)}, bf16[2,512,4,64]{1,3,2,0:T(8,128)(2,1)}, f32[2,4,512]{2,1,0:T(4,128)S(1)}, s32[2]{0:T(128)S(1)}, s32[1024]{0:T(1024)S(1)}, /*index=...) while((s32[]{:T(128)}, ...), condition=%wide.region_7.8_spmd, body=%wide.region_4.7_spmd.sunk | while | flops 565312512 | bytes 33111288 | solution.py:114
  89.6 15.1 %all-to-all-start = ((bf16[4,256,256]{1,2,0:T(8,128)(2,1)}), bf16[4,256,256]{1,2,0:T(8,128)(2,1)S(1)}, u32[]{:S(2)}, u32[]{:S(2)}) async-start(bf16[4,256,256]{1,2,0:T(8,128)(2,1)} %copy.96), calls=%async_computation | async-start | bytes 1048576 | tf_op jit(solution)/shard_map/all_to_all | solution.py:446
  113.0 20.3 %maximum_maximum_fusion = bf16[8,128,3072]{1,2,0:T(8,128)(2,1)} fusion(bf16[4,128,1024]{1,2,0:T(8,128)(2,1)S(1)} %copy-done.25, bf16[4,128,2048]{1,2,0:T(8,128)(2,1)S(1)} %bitcast.239), kind=kLoop, calls=%fused_computation.60 | loop fusion | flops 25165824 | bytes 9437184 | tf_op jit(solution)/shard_map/concatenate | solution.py:419
  133.3 4.9 all-to-all-start.1
  139.8 51.8 %all-gather.5.cloned.1.call-done = bf16[1024,1024]{1,0:T(8,128)(2,1)} async-done(((bf16[128,1024]{1,0:T(8,128)(2,1)}), bf16[1024,1024]{1,0:T(8,128)(2,1)}) %all-gather.5.cloned.1.call-update) | async-done | bytes 2097168 | tf_op jit(solution)/shard_map/all_gather | solution.py:410
  197.4 32.7 %shard_map.204 = bf16[1024,1024]{1,0:T(8,128)(2,1)} custom-call(bf16[256,1024]{1,0:T(8,128)(2,1)} %multiply_convert_fusion.9.own_ref), custom_call_target="tpu_custom_call" | custom-call | bytes 52428800 | tf_op jit(solution)/shard_map/pallas_call | solution.py:273
  230.1 4.4 slice.135
  234.5 6.5 %copy.100 = bf16[8,128,2048]{2,1,0:T(8,128)(2,1)} copy(bf16[8,128,2048]{1,2,0:T(8,128)(2,1)} %slice.135) | data formatting | bytes 8388608 | tf_op jit(solution)/shard_map/slice | solution.py:421
  248.0 6.9 %fusion.60 = f32[1024,2048]{1,0:T(8,128)S(1)} fusion(bf16[1024,1024]{1,0:T(8,128)(2,1)} %shard_map.204, bf16[1024,2048]{1,0:T(8,128)(2,1)} %bitcast.244), kind=kOutput, calls=%fused_computation.173 | convolution fusion | flops 4294967296 | bytes 14680064 | tf_op jit(solution)/shard_map/dot_general | solution.py:453
  262.1 18.5 %shard_map.205 = f32[256,1024]{1,0:T(8,128)} custom-call(bf16[4,256,1024]{2,1,0:T(8,128)(2,1)} %bitcast.249), custom_call_target="tpu_custom_call" | custom-call | bytes 52428800 | tf_op jit(solution)/shard_map/pallas_call | solution.py:351
  288.5 17.7 %shard_map.206 = bf16[1024,1024]{1,0:T(8,128)(2,1)} custom-call(bf16[256,1024]{1,0:T(8,128)(2,1)} %multiply_convert_fusion.5.own_ref), custom_call_target="tpu_custom_call" | custom-call | bytes 52428800 | tf_op jit(solution)/shard_map/pallas_call | solution.py:273
  306.2 9.6 %multiply_reduce_fusion.1 = (f32[1024]{0:T(1024)}, f32[1024]{0:T(1024)}, f32[1024,1024]{1,0:T(8,128)S(1)}, bf16[1024,1024]{1,0:T(8,128)(2,1)S(1)}) fusion(f32[1024,2048]{1,0:T(8,128)} %copy-done.20, f32[1024]{0:T(1024)S(1)} %bitcast.277, f32[1024]{0:T(1024)S(1)} %bitcast.280, bf16[1024,1024]{1,0:T(8,128)(2,1)} %shard_map.206, bf16[1024,1024]{1,0:T(8,128)(2,1)} %bitcast.252), kind=kOutput, calls=%fused_computation.63 | convolution fusion | flops 2167404544 | bytes 18890752 | tf_op jit(solution)/shard_map/dot_general | solution.py:39
  318.0 5.8 fusion.49
  323.9 6.4 %convolution_convert_fusion = bf16[1024,2048]{1,0:T(8,128)(2,1)} fusion(bf16[1024,1024]{1,0:T(8,128)(2,1)S(1)} %copy-done.28, bf16[1024,1024]{1,0:T(8,128)(2,1)S(1)} %multiply_convert_fusion.1, bf16[1024,1024]{1,0:T(8,128)(2,1)S(1)} %get-tuple-element.334), kind=kOutput, calls=%fused_computation.74 | convolution fusion | flops 4305453056 | bytes 10485760 | tf_op jit(solution)/shard_map/dot_general | solution.py:33
  330.3 18.5 %shard_map.207 = f32[256,1024]{1,0:T(8,128)} custom-call(bf16[4,256,1024]{2,1,0:T(8,128)(2,1)} %bitcast.248), custom_call_target="tpu_custom_call" | custom-call | bytes 52428800 | tf_op jit(solution)/shard_map/pallas_call | solution.py:351
  361.5 5.1 all-to-all-start.2
  367.4 4.8 convolution_convert_fusion.1
  375.4 5.8 all-to-all-done.2
  381.1 4.8 all-to-all-start.5
  390.1 57.7 %while.28 = (s32[]{:T(128)}, f32[1024,4,64]{0,2,1:T(8,128)S(1)}, f32[1024,4,64]{0,2,1:T(8,128)}, f32[2,512,4,64]{1,0,3,2:T(2,128)}, bf16[2,512,4,64]{1,3,2,0:T(8...) while((s32[]{:T(128)}, f32[1024,4,64]{0,2,1:T(8,128)S(1)}, ...), condition=%wide.region_18.19_spmd.clone, body=%wide.region_16.18_spmd.clone.sunk | while | flops 1378221056 | bytes 82910512 | solution.py:160
  398.7 4.6 multiply_reduce_fusion.17
  408.6 10.4 %dynamic_update_slice.32 = f32[2,512,4,64]{1,0,3,2:T(2,128)} dynamic-update-slice(f32[2,512,4,64]{1,0,3,2:T(2,128)} %get-tuple-element.564, f32[1,512,4,64]{1,0,3,2:T(1,128)S(1)} %copy.141, s32[]{:T(128)S(6)} %copy.158, s32[]{:T(128)} %constant.62.clone.1..sunk.1, s32[]{:T(128)} %constant.62.clone.1..sunk.1, s32[]{:T(128)} %constant.62.clone.1..sunk.1) | dynamic-update-slice | bytes 1048580 | tf_op jit(solution)/shard_map/while/body/jit(dynamic_update_index_in_dim)/dynamic_update_slice | solution.py:160
  427.5 4.6 multiply_reduce_fusion.17
  437.4 10.4 %dynamic_update_slice.32 = f32[2,512,4,64]{1,0,3,2:T(2,128)} dynamic-update-slice(f32[2,512,4,64]{1,0,3,2:T(2,128)} %get-tuple-element.564, f32[1,512,4,64]{1,0,3,2:T(1,128)S(1)} %copy.141, s32[]{:T(128)S(6)} %copy.158, s32[]{:T(128)} %constant.62.clone.1..sunk.1, s32[]{:T(128)} %constant.62.clone.1..sunk.1, s32[]{:T(128)} %constant.62.clone.1..sunk.1) | dynamic-update-slice | bytes 1048580 | tf_op jit(solution)/shard_map/while/body/jit(dynamic_update_index_in_dim)/dynamic_update_slice | solution.py:160
  465.9 6.9 %reduce_sum.205 = bf16[4,128,3072]{2,1,0:T(8,128)(2,1)} reduce(bf16[2,4,128,3072]{3,2,1,0:T(8,128)(2,1)} %bitcast.51, bf16[]{:T(256)} %constant.63.clone.1), dimensions={0}, to_apply=%region_25.26 | reduce | flops 1572864 | bytes 9437186 | tf_op jit(solution)/shard_map/reduce_sum | solution.py:489
  483.9 17.9 %reduce-scatter.16.cloned.1.call-done = bf16[128,768]{1,0:T(8,128)(2,1)} async-done(((bf16[1024,768]{1,0:T(8,128)(2,1)}), bf16[128,768]{1,0:T(8,128)(2,1)}) %reduce-scatter.16.cloned.1.call-update) | async-done | bytes 196624 | tf_op jit(solution)/shard_map/reduce_scatter | solution.py:533
  501.7 4.6 all-to-all-start.4
  506.3 4.6 convolution_convert_fusion.4
  515.0 4.6 all-to-all-start.3
  520.3 84.1 %all-reduce = f32[32,352]{1,0:T(8,128)S(1)} all-reduce(f32[32,352]{1,0:T(8,128)S(1)} %concatenate.64), channel_id=7, replica_groups=mesh['dp'=8,'seq'=4] {'dp','seq'}, use_global_device_ids=true, to_apply=%region_33.34.clone | all-reduce | flops 11264 | bytes 90112
  613.6 11.1 %reduce-scatter.18.cloned.1.call-done = bf16[32,8192]{1,0:T(8,128)(2,1)} async-done(((bf16[128,8192]{1,0:T(8,128)(2,1)}), bf16[32,8192]{1,0:T(8,128)(2,1)}) %reduce-scatter.18.cloned.1.call-update) | async-done | bytes 524304 | tf_op jit(solution)/shard_map/reduce_scatter | solution.py:493
  (294 shorter events, 168.1 us)
Async XLA Ops:
  7.2 46.1 %all-gather.3.cloned.1.call-start = ((), (), s32[]{:S(2)}) async-start(), calls=%async_computation.11 | async-start | bytes 1769472 | tf_op jit(solution)/shard_map/all_gather | solution.py:409
  10.3 50.7 %copy-start.49 = (f32[4,64]{1,0:T(4,128)}, f32[4,64]{1,0:T(4,128)S(1)}, u32[]{:S(2)}) copy-start(f32[4,64]{1,0:T(4,128)S(1)} %mul.500) | copy-start | bytes 3076
  86.8 24.3 %copy-start.4 = (bf16[1024,4,64]{0,2,1:T(8,128)(2,1)}, bf16[1024,4,64]{0,2,1:T(8,128)(2,1)S(1)}, u32[]{:S(2)}) copy-start(bf16[1024,4,64]{0,2,1:T(8,128)(2,1)S(1)} %get-tuple-element.604) | copy-start | bytes 1572868
  89.6 43.7 %all-to-all-start = ((bf16[4,256,256]{1,2,0:T(8,128)(2,1)}), bf16[4,256,256]{1,2,0:T(8,128)(2,1)S(1)}, u32[]{:S(2)}, u32[]{:S(2)}) async-start(bf16[4,256,256]{1,2,0:T(8,128)(2,1)} %copy.96), calls=%async_computation | async-start | bytes 1048576 | tf_op jit(solution)/shard_map/all_to_all | solution.py:446
  133.3 6.5 %copy-start.44 = (f32[1024]{0:T(1024)S(1)}, f32[1024]{0:T(1024)}, u32[]{:S(2)}) copy-start(f32[1024]{0:T(1024)} %param.26) | copy-start | bytes 12292
  133.3 61.7 %copy-start.51 = (f32[1024]{0:T(1024)S(1)}, f32[1024]{0:T(1024)}, u32[]{:S(2)}) copy-start(f32[1024]{0:T(1024)} %param.25) | copy-start | bytes 12292
  133.3 58.3 %copy-start.22 = (bf16[4,256,256]{1,2,0:T(8,128)(2,1)}, bf16[4,256,256]{1,2,0:T(8,128)(2,1)S(1)}, u32[]{:S(2)}) copy-start(bf16[4,256,256]{1,2,0:T(8,128)(2,1)S(1)} %all-to-all-done) | copy-start | bytes 1572868
  133.3 96.8 %all-to-all-start.1 = ((bf16[8,128,3072]{1,2,0:T(8,128)(2,1)}), bf16[8,128,3072]{1,2,0:T(8,128)(2,1)}, u32[]{:S(2)}, u32[]{:S(2)}) async-start(bf16[8,128,3072]{1,2,0:T(8,128)(2,1)} %maximum_maximum_fusion), calls=%async_computation.1 | async-start | bytes 12582912 | tf_op jit(solution)/shard_map/all_to_all | solution.py:420
  138.2 56.8 %copy-start.21 = (bf16[1,256,1024]{2,1,0:T(8,128)(2,1)S(1)}, bf16[1,256,1024]{2,1,0:T(8,128)(2,1)}, u32[]{:S(2)}) copy-start(bf16[1,256,1024]{2,1,0:T(8,128)(2,1)} %param.16) | copy-start | bytes 1572868
  138.2 53.4 %all-gather.5.cloned.1.call-start = ((), (), s32[]{:S(2)}) async-start(), calls=%async_computation.12 | async-start | bytes 2359296 | tf_op jit(solution)/shard_map/all_gather | solution.py:410
  280.7 5.7 copy-start
  280.7 5.7 copy-start.2
  280.7 5.7 copy-start.8
  318.0 5.8 copy-start.28
  361.5 19.6 %all-to-all-start.2 = ((bf16[256,4,256]{0,2,1:T(8,128)(2,1)}), bf16[256,4,256]{0,2,1:T(8,128)(2,1)S(1)}, u32[]{:S(2)}, u32[]{:S(2)}) async-start(bf16[256,4,256]{0,2,1:T(8,128)(2,1)} %bitcast.37), calls=%async_computation.2 | async-start | bytes 1048576 | tf_op jit(solution)/shard_map/all_to_all | solution.py:518
  366.6 97.2 %reduce-scatter.10.cloned.1.call-start = ((), (), s32[]{:S(2)}) async-start(), calls=%async_computation.13 | async-start | bytes 2359296 | tf_op jit(solution)/shard_map/reduce_scatter | solution.py:513
  375.4 14.8 %copy-start.5 = (bf16[1024,4,64]{0,2,1:T(8,128)(2,1)S(1)}, bf16[1024,4,64]{0,2,1:T(8,128)(2,1)}, u32[]{:S(2)}) copy-start(bf16[1024,4,64]{0,2,1:T(8,128)(2,1)} %copy-done.4) | copy-start | bytes 1572868
  381.1 84.8 %all-to-all-start.5 = ((bf16[8,128,3072]{2,1,0:T(8,128)(2,1)}), bf16[8,128,3072]{2,1,0:T(8,128)(2,1)}, u32[]{:S(2)}, u32[]{:S(2)}) async-start(bf16[8,128,3072]{2,1,0:T(8,128)(2,1)} %pad_maximum_fusion), calls=%async_computation.7 | async-start | bytes 12582912 | tf_op jit(solution)/shard_map/all_to_all | solution.py:486
  385.9 115.8 %reduce-scatter.16.cloned.1.call-start = ((), (), s32[]{:S(2)}) async-start(), calls=%async_computation.16 | async-start | bytes 1769472 | tf_op jit(solution)/shard_map/reduce_scatter | solution.py:533
  390.1 61.0 %copy-start.46 = (f32[2,512,4]{1,0,2:T(2,128)S(1)}, f32[2,512,4]{1,0,2:T(2,128)}, u32[]{:S(2)}) copy-start(f32[2,512,4]{1,0,2:T(2,128)} %copy-done.45) | copy-start | bytes 49156
  390.1 61.0 %copy-start.50 = (f32[4,64]{1,0:T(4,128)S(1)}, f32[4,64]{1,0:T(4,128)}, u32[]{:S(2)}) copy-start(f32[4,64]{1,0:T(4,128)} %copy-done.49) | copy-start | bytes 3076
  447.8 5.7 copy-start.19
  463.8 143.2 %reduce-scatter.12.cloned.1.call-start = ((), (), s32[]{:S(2)}) async-start(), calls=%async_computation.14 | async-start | bytes 327680 | tf_op jit(solution)/shard_map/reduce_scatter | solution.py:512
  464.4 147.4 %reduce-scatter.14.cloned.1.call-start = ((), (), s32[]{:S(2)}) async-start(), calls=%async_computation.15 | async-start | bytes 1310720 | tf_op jit(solution)/shard_map/reduce_scatter | solution.py:500
  475.2 149.6 %reduce-scatter.18.cloned.1.call-start = ((), (), s32[]{:S(2)}) async-start(), calls=%async_computation.17 | async-start | bytes 2621440 | tf_op jit(solution)/shard_map/reduce_scatter | solution.py:493
  479.6 26.7 %copy-start.32 = (bf16[1024,3,4,64]{0,3,2,1:T(8,128)(2,1)S(1)}, bf16[1024,3,4,64]{0,3,2,1:T(8,128)(2,1)}, u32[]{:S(2)}) copy-start(bf16[1024,3,4,64]{0,3,2,1:T(8,128)(2,1)} %copy-done.31) | copy-start | bytes 4718596
  501.7 13.3 %all-to-all-start.4 = ((bf16[4,32,768]{2,1,0:T(8,128)(2,1)}), bf16[4,32,768]{2,1,0:T(8,128)(2,1)S(1)}, u32[]{:S(2)}, u32[]{:S(2)}) async-start(bf16[4,32,768]{2,1,0:T(8,128)(2,1)} %bitcast.272), calls=%async_computation.4 | async-start | bytes 393216 | tf_op jit(solution)/shard_map/all_to_all | solution.py:534
  510.9 8.8 %copy-start.52 = (f32[1024]{0:T(1024)S(1)}, f32[1024]{0:T(1024)}, u32[]{:S(2)}) copy-start(f32[1024]{0:T(1024)} %get-tuple-element.274) | copy-start | bytes 12292
  510.9 8.8 %copy-start.54 = (f32[1024]{0:T(1024)S(1)}, f32[1024]{0:T(1024)}, u32[]{:S(2)}) copy-start(f32[1024]{0:T(1024)} %get-tuple-element.272) | copy-start | bytes 12292
  510.9 8.9 %copy-start.53 = (f32[1024]{0:T(1024)S(1)}, f32[1024]{0:T(1024)}, u32[]{:S(2)}) copy-start(f32[1024]{0:T(1024)} %get-tuple-element.273) | copy-start | bytes 12292
  515.0 95.6 %copy-start.14 = (f32[256,1024]{1,0:T(8,128)S(1)}, f32[256,1024]{1,0:T(8,128)}, u32[]{:S(2)}) copy-start(f32[256,1024]{1,0:T(8,128)} %copy-done.13) | copy-start | bytes 3145732
  515.0 93.5 %all-to-all-start.3 = ((bf16[4,256,1024]{2,1,0:T(8,128)(2,1)}), bf16[4,256,1024]{2,1,0:T(8,128)(2,1)}, u32[]{:S(2)}, u32[]{:S(2)}) async-start(bf16[4,256,1024]{2,1,0:T(8,128)(2,1)} %bitcast.251), calls=%async_computation.3 | async-start | bytes 4194304 | tf_op jit(solution)/shard_map/all_to_all | solution.py:544
  (40 other events, 127.3 us)
Sparse Core Ops, SparseCore 0:
  10.4 28.4 all-gather.2
  140.9 50.6 all-gather.4
  370.7 65.3 reduce-scatter.9
  463.9 37.7 reduce-scatter.15
  503.8 19.9 reduce-scatter.11
  526.5 51.4 reduce-scatter.13
  580.3 44.3 reduce-scatter.17

commit v3 on v2

--- a/solution.py
+++ b/solution.py
@@ -367,6 +367,145 @@
         ),
         compiler_params=pltpu.CompilerParams(collective_id=2, has_side_effects=True),
     )(part)
+
+
+def seq_swap_kernel(to_tokens, count, part_ref, out_ref, send_sem, recv_sem, local_sem):
+    rows = part_ref.shape[0] // count if to_tokens else part_ref.shape[0]
+    width = part_ref.shape[1] if to_tokens else part_ref.shape[1] // count
+    mine = lax.axis_index("seq")
+    peers = [lax.rem(mine + step, count) for step in range(1, count)]
+    greet([{"seq": peer} for peer in peers])
+
+    def by_rows(ref, index):
+        return ref.at[pl.ds(pl.multiple_of(index * rows, rows), rows), :]
+
+    def by_columns(ref, index):
+        return ref.at[:, pl.ds(pl.multiple_of(index * width, width), width)]
+
+    take, give = (by_rows, by_columns) if to_tokens else (by_columns, by_rows)
+    copies = [
+        pltpu.make_async_remote_copy(
+            src_ref=take(part_ref, peer),
+            dst_ref=give(out_ref, mine),
+            send_sem=send_sem.at[slot],
+            recv_sem=recv_sem.at[slot],
+            device_id={"seq": peer},
+            device_id_type=MESH_ID,
+        )
+        for slot, peer in enumerate(peers)
+    ]
+    for copy in copies:
+        copy.start()
+    local = pltpu.make_async_copy(take(part_ref, mine), give(out_ref, mine), local_sem)
+    local.start()
+    local.wait()
+    for copy in copies:
+        copy.wait()
+
+
+def seq_swap(part, to_tokens):
+    count = lax.axis_size("seq")
+    rows, width = part.shape
+    shape = (rows // count, width * count) if to_tokens else (rows * count, width // count)
+    return pl.pallas_call(
+        functools.partial(seq_swap_kernel, to_tokens, count),
+        out_shape=jax.ShapeDtypeStruct(shape, part.dtype),
+        in_specs=[pl.BlockSpec(memory_space=pltpu.VMEM)],
+        out_specs=pl.BlockSpec(memory_space=pltpu.VMEM),
+        scratch_shapes=[
+            pltpu.SemaphoreType.DMA((count - 1,)),
+            pltpu.SemaphoreType.DMA((count - 1,)),
+            pltpu.SemaphoreType.DMA,
+        ],
+        cost_estimate=pl.CostEstimate(
+            flops=0, bytes_accessed=100 * rows * width, transcendentals=0
+        ),
+        compiler_params=pltpu.CompilerParams(
+            collective_id=3 if to_tokens else 4, has_side_effects=True
+        ),
+    )(part)
+
+
+def seq_sum_kernel(count, part_ref, base_ref, out_ref, landed, send_sem, recv_sem):
+    mine = lax.axis_index("seq")
+    peers = [lax.rem(mine + step, count) for step in range(1, count)]
+    greet([{"seq": peer} for peer in peers])
+    copies = [
+        pltpu.make_async_remote_copy(
+            src_ref=part_ref.at[peer],
+            dst_ref=landed.at[slot],
+            send_sem=send_sem.at[slot],
+            recv_sem=recv_sem.at[slot],
+            device_id={"seq": peer},
+            device_id_type=MESH_ID,
+        )
+        for slot, peer in enumerate(peers)
+    ]
+    for copy in copies:
+        copy.start()
+    out_ref[...] = base_ref[...] + part_ref[mine].astype(jnp.float32)
+    for slot, copy in enumerate(copies):
+        copy.wait_recv()
+        out_ref[...] = out_ref[...] + landed[slot].astype(jnp.float32)
+    for copy in copies:
+        copy.wait_send()
+
+
+def seq_sum(part, base):
+    count, rows, width = part.shape
+    return pl.pallas_call(
+        functools.partial(seq_sum_kernel, count),
+        out_shape=jax.ShapeDtypeStruct((rows, width), jnp.float32),
+        in_specs=[pl.BlockSpec(memory_space=pltpu.VMEM)] * 2,
+        out_specs=pl.BlockSpec(memory_space=pltpu.VMEM),
+        scratch_shapes=[
+            pltpu.VMEM((count - 1, rows, width), part.dtype),
+            pltpu.SemaphoreType.DMA((count - 1,)),
+            pltpu.SemaphoreType.DMA((count - 1,)),
+        ],
+        cost_estimate=pl.CostEstimate(
+            flops=0, bytes_accessed=100 * count * rows * width, transcendentals=0
+        ),
+        compiler_params=pltpu.CompilerParams(collective_id=5, has_side_effects=True),
+    )(part, base)
+
+
+def pack_kernel(in_ref, down_ref, in_out, down_out):
+    depth = down_out.shape[1]
+    places = in_out.shape[0]
+    for rank in range(TEAM):
+        for part in range(in_out.shape[2] // depth):
+            first = (part * TEAM + rank) * depth
+            values = in_ref[:, first : first + depth]
+            for place in range(rank, places, TEAM):
+                in_out[place, :, part * depth : (part + 1) * depth] = values
+        values = down_ref[rank * depth : (rank + 1) * depth, :]
+        for place in range(rank, places, TEAM):
+            down_out[place] = values
+
+
+def pack_ff(w_in, w_down, dp_count, ff_part):
+    in_rows, in_cols = w_in.shape
+    model_width = w_down.shape[1]
+    if ff_part % 128 == 0 and in_rows == ff_part:
+        return pl.pallas_call(
+            pack_kernel,
+            out_shape=(
+                jax.ShapeDtypeStruct((dp_count, in_rows, in_cols // TEAM), w_in.dtype),
+                jax.ShapeDtypeStruct((dp_count, ff_part, model_width), w_in.dtype),
+            ),
+            in_specs=[pl.BlockSpec(memory_space=pltpu.VMEM)] * 2,
+            out_specs=(
+                pl.BlockSpec(memory_space=pltpu.VMEM),
+                pl.BlockSpec(memory_space=pltpu.VMEM),
+            ),
+            cost_estimate=pl.CostEstimate(flops=0, bytes_accessed=1 << 23, transcendentals=0),
+        )(w_in, w_down)
+    copies = dp_count // TEAM
+    in_parts = w_in.reshape(in_rows, 2 * dp_count, TEAM, ff_part).transpose(2, 0, 1, 3)
+    in_blocks = jnp.concatenate([in_parts.reshape(TEAM, in_rows, in_cols // TEAM)] * copies)
+    down_blocks = jnp.concatenate([w_down.reshape(TEAM, ff_part, model_width)] * copies)
+    return in_blocks, down_blocks
 
 
 def body(
@@ -406,20 +545,20 @@
     head_cols = lax.dynamic_slice_in_dim(
         w_qkv.reshape(-1, 3, model_width), offset, group_width, axis=2
     ).reshape(-1, 3 * group_width)
-    heads_qkv = lax.all_gather(head_cols, "dp", axis=0, tiled=True)
-    full_out = lax.all_gather(w_attn_out, "dp", axis=0, tiled=True)
-    in_parts = w_in.reshape(in_rows, 2 * dp_count, TEAM, ff_part).transpose(2, 0, 1, 3)
-    ff_blocks = jnp.concatenate(
-        [
-            in_parts.reshape(TEAM, in_rows, 2 * ff_team),
-            w_down.reshape(TEAM, ff_part, model_width),
-        ],
-        axis=2,
-    )
-    ff_blocks = jnp.concatenate([ff_blocks] * (dp_count // TEAM), axis=0)
-    team_ff = lax.all_to_all(ff_blocks, "dp", 0, 0, tiled=True)
-    team_in = team_ff[:, :, : 2 * ff_team].reshape(model_width, 2 * ff_team)
-    team_down = team_ff[:, :, 2 * ff_team :].reshape(ff_team, model_width)
+    gathered = lax.all_gather(
+        jnp.concatenate([head_cols, w_attn_out], axis=1), "dp", axis=0, tiled=True
+    )
+    heads_qkv = gathered[:, : 3 * group_width]
+    full_out = gathered[:, 3 * group_width :]
+    in_blocks, down_blocks = pack_ff(w_in, w_down, dp_count, ff_part)
+    seq_tokens = seq_gather(inputs_b)
+    in_blocks, down_blocks, seq_tokens = lax.optimization_barrier(
+        (in_blocks, down_blocks, seq_tokens)
+    )
+    team_in = lax.all_to_all(in_blocks, "dp", 0, 0, tiled=True)
+    team_down = lax.all_to_all(down_blocks, "dp", 0, 0, tiled=True)
+    team_in = team_in.reshape(model_width, 2 * ff_team)
+    team_down = team_down.reshape(ff_team, model_width)
 
     def team_slice(scale):
         return lax.dynamic_index_in_dim(
@@ -428,7 +567,6 @@
 
     s_u_team, s_v_team = team_slice(s_u), team_slice(s_v)
 
-    seq_tokens = seq_gather(inputs_b)
     by_heads = (
         jnp.dot(seq_tokens, heads_qkv, preferred_element_type=jnp.float32)
         .astype(jnp.bfloat16)
@@ -443,7 +581,7 @@
     )
     value_b = by_heads[:, 2].reshape(length, head_group, HD)
     attn_mixed, log_sums = attend_forward(query_n, key_n, value_b, seg_row, score_scale)
-    attn_pieces = lax.all_to_all(attn_mixed, "seq", split_axis=0, concat_axis=1, tiled=True)
+    attn_pieces = seq_swap(attn_mixed, True)
     attn_proj = jnp.dot(attn_pieces, full_out, preferred_element_type=jnp.float32)
     attn_unit, attn_inv = rms_norm(attn_proj)
     hidden, hidden_inv = rms_norm(inputs_f + alpha_attn * (attn_unit - inputs_f))
@@ -480,44 +618,55 @@
     hidden_part = contract_cols(grad_up_gate, team_in)
     hidden_sum = team_sum(hidden_part.astype(jnp.bfloat16).reshape(TEAM, local_rows, model_width))
     grad_hidden = (1.0 - alpha_mlp) * grad_two + hidden_sum
-    grad_w_ff = jnp.concatenate(
-        [contract_rows(team_hidden, grad_up_gate), contract_rows(inner_act, team_grad)], axis=1
+    in_terms = contract_rows(team_hidden, grad_up_gate).astype(jnp.bfloat16)
+    down_terms = contract_rows(inner_act, team_grad).astype(jnp.bfloat16)
+    ff_terms = jnp.concatenate(
+        [
+            in_terms[:, :ff_team].reshape(dp_count, in_rows, ff_team),
+            in_terms[:, ff_team:].reshape(dp_count, in_rows, ff_team),
+            down_terms.reshape(dp_count, in_rows, model_width),
+        ],
+        axis=1,
+    )
+    ff_terms = lax.all_to_all(ff_terms, "dp", 0, 0, tiled=True)
+    ff_sums = jnp.sum(
+        ff_terms.reshape(dp_count // TEAM, TEAM, 3, in_rows, model_width).astype(jnp.float32),
+        axis=0,
     ).astype(jnp.bfloat16)
-    ff_terms = lax.all_to_all(
-        grad_w_ff.reshape(dp_count, in_rows, 2 * ff_team + model_width), "dp", 0, 0, tiled=True
-    )
-    ff_sums = jnp.sum(
-        ff_terms.reshape(dp_count // TEAM, TEAM, in_rows, -1).astype(jnp.float32), axis=0
-    ).astype(jnp.bfloat16)
-    in_sums = ff_sums[:, :, : 2 * ff_team].transpose(1, 0, 2).reshape(in_rows, 2 * ff_width)
-    shard_w_in = lax.psum_scatter(in_sums, "seq", scatter_dimension=0, tiled=True)
-    shard_w_in = (
-        shard_w_in.reshape(-1, TEAM, 2 * dp_count, ff_part)
-        .transpose(0, 2, 1, 3)
-        .reshape(-1, 2 * ff_width)
-        .astype(jnp.float32)
-    )
-    shard_w_down = lax.psum_scatter(
-        ff_sums[:, :, 2 * ff_team :].reshape(TEAM * ff_part, model_width),
-        "seq",
-        scatter_dimension=0,
-        tiled=True,
-    ).astype(jnp.float32)
+    out_rows = in_rows // seq_count
+    in_sums = (
+        ff_sums[:, :2]
+        .reshape(TEAM, 2, seq_count, out_rows, model_width)
+        .transpose(2, 0, 1, 3, 4)
+        .reshape(seq_count, TEAM * 2 * out_rows, model_width)
+    )
+    down_sums = ff_sums[:, 2].reshape(seq_count, -1, model_width)
 
     grad_one = rms_back(grad_hidden, hidden, hidden_inv)
     grad_alpha_attn = jnp.sum(grad_one * (attn_unit - inputs_f), axis=0)
     grad_attn_proj = rms_back(alpha_attn * grad_one, attn_unit, attn_inv).astype(jnp.bfloat16)
     grad_pieces = contract_cols(grad_attn_proj, full_out).astype(jnp.bfloat16)
     grad_w_attn_out = contract_rows(attn_pieces, grad_attn_proj).astype(jnp.bfloat16)
-    shard_w_attn_out = lax.psum_scatter(
-        lax.psum_scatter(grad_w_attn_out, "dp", scatter_dimension=0, tiled=True),
+    out_sums = lax.psum_scatter(
+        grad_w_attn_out, "dp", scatter_dimension=0, tiled=True
+    ).reshape(seq_count, out_rows, model_width)
+    shards = lax.psum_scatter(
+        jnp.concatenate([in_sums, down_sums, out_sums], axis=1).reshape(-1, model_width),
         "seq",
         scatter_dimension=0,
         tiled=True,
-    ).astype(jnp.float32)
-    grad_heads = lax.all_to_all(
-        grad_pieces, "seq", split_axis=1, concat_axis=0, tiled=True
-    ).reshape(length, head_group, HD)
+    )
+    in_span = TEAM * 2 * out_rows
+    shard_w_in = (
+        shards[:in_span]
+        .reshape(TEAM, 2, out_rows, dp_count, ff_part)
+        .transpose(2, 1, 3, 0, 4)
+        .reshape(out_rows, 2 * ff_width)
+        .astype(jnp.float32)
+    )
+    shard_w_down = shards[in_span:-out_rows].astype(jnp.float32)
+    shard_w_attn_out = shards[-out_rows:].astype(jnp.float32)
+    grad_heads = seq_swap(grad_pieces, False).reshape(length, head_group, HD)
     grad_query_n, grad_key_n, grad_value = attend_backward(
         query_n, key_n, value_b, grad_heads, log_sums, seg_row, score_scale
     )
@@ -529,24 +678,6 @@
         .reshape(length, 3 * group_width)
         .astype(jnp.bfloat16)
     )
-    grad_w_qkv = contract_rows(seq_tokens, grad_qkv).astype(jnp.bfloat16)
-    rows_w_qkv = lax.psum_scatter(grad_w_qkv, "dp", scatter_dimension=0, tiled=True)
-    shard_w_qkv = lax.all_to_all(
-        rows_w_qkv.reshape(seq_count, -1, 3 * group_width), "seq", 0, 0, tiled=True
-    )
-    shard_w_qkv = (
-        shard_w_qkv.reshape(seq_count, -1, 3, group_width)
-        .transpose(1, 2, 0, 3)
-        .reshape(-1, 3 * model_width)
-        .astype(jnp.float32)
-    )
-    tokens_part = contract_cols(grad_qkv, heads_qkv).astype(jnp.bfloat16)
-    tokens_terms = lax.all_to_all(
-        tokens_part.reshape(seq_count, local_rows, model_width), "seq", 0, 0, tiled=True
-    )
-    grad_inputs = (1.0 - alpha_attn) * grad_one + jnp.sum(
-        tokens_terms.astype(jnp.float32), axis=0
-    )
 
     def team_spread(part):
         whole = jnp.zeros((dp_count, TEAM, ff_part), jnp.float32)
@@ -564,10 +695,42 @@
         grad_alpha_attn,
         grad_alpha_mlp,
     )
+    grad_w_qkv = contract_rows(seq_tokens, grad_qkv).astype(jnp.bfloat16)
+    small_count = sum(term.shape[0] for term in small_terms) // (dp_count * seq_count)
+    small_rows = 8 * -(-small_count // (24 * group_width))
     packed = jnp.concatenate(
-        [term.reshape(dp_count * seq_count, -1) for term in small_terms], axis=1
-    )
-    packed = lax.psum_scatter(packed, ("dp", "seq"), scatter_dimension=0, tiled=True).reshape(-1)
+        [term.reshape(dp_count, seq_count, -1) for term in small_terms], axis=2
+    ).astype(jnp.bfloat16)
+    packed = jnp.pad(packed, ((0, 0), (0, 0), (0, small_rows * 3 * group_width - small_count)))
+    packed = jnp.concatenate(
+        [
+            grad_w_qkv.reshape(dp_count, seq_count, out_rows, 3 * group_width),
+            packed.reshape(dp_count, seq_count, small_rows, 3 * group_width),
+        ],
+        axis=2,
+    )
+    span = out_rows + small_rows
+    packed = lax.psum_scatter(
+        packed.reshape(dp_count * seq_count * span, 3 * group_width),
+        "dp",
+        scatter_dimension=0,
+        tiled=True,
+    )
+    tokens_part = contract_cols(grad_qkv, heads_qkv).astype(jnp.bfloat16)
+    grad_inputs = seq_sum(
+        tokens_part.reshape(seq_count, local_rows, model_width), (1.0 - alpha_attn) * grad_one
+    )
+    packed = lax.all_to_all(
+        packed.reshape(seq_count, span, 3 * group_width), "seq", 0, 0, tiled=True
+    )
+    shard_w_qkv = (
+        packed[:, :out_rows]
+        .reshape(seq_count, -1, 3, group_width)
+        .transpose(1, 2, 0, 3)
+        .reshape(-1, 3 * model_width)
+        .astype(jnp.float32)
+    )
+    packed = jnp.sum(packed[:, out_rows:].astype(jnp.float32), axis=0).reshape(-1)
     small_shards = []
     spot = 0
     for term in small_terms:
@@ -599,6 +762,7 @@
         P(),
         P("dp", "seq", None),
     )
+
     return jax.shard_map(
         body,
         mesh=mesh,

time: 646 us -> 663 us (1.026)
  the two profiles are of different devices: /device:TPU:0 before, /device:TPU:9 now
where the time goes in v3:
time: 663 us; the launch traced here: 650 us
  Pallas kernels  343 us (52%)
  matrix products  91.7 us (14%)
  local copies, waits for them, and re-layouts  71.8 us (11%)
  other arithmetic  69.6 us (10%)
  waiting for transfers between devices  31 us (5%)
  starting transfers between devices  20 us (3%)
  between operations  15 us (2%)
  loops' own time  8.48 us (1%)
    pallas_call x2, Pallas kernels, team_sum(): pl.pallas_call(team_sum_kernel, out_shape=jax.ShapeDtypeStruct((rows, wid...  100 us
    pallas_call x1, Pallas kernels, seq_sum(): pl.pallas_call(functools.partial(seq_sum_kernel, count), out_shape=jax.Sh...  99.2 us
    pallas_call x2, Pallas kernels, team_gather(): pl.pallas_call(team_gather_kernel, out_shape=jax.ShapeDtypeStruct((TEAM *...  55.4 us
    pallas_call x1, Pallas kernels, seq_gather(): pl.pallas_call(functools.partial(seq_gather_kernel, count), out_shape=jax...  49 us
    pallas_call x2, Pallas kernels, seq_swap(): pl.pallas_call(functools.partial(seq_swap_kernel, to_tokens, count), out_...  33.4 us
    reduce_scatter x1, waiting for transfers between devices, body(): lax.psum_scatter(packed.reshape(dp_count * seq_count * span, 3 * group_wi...  28.6 us
    dot_general x4, matrix products, contract_cols(): lax.dot_general(left_arr, right_arr, (((1,), (1,)), ((), ())), preferred_...  25.5 us
    dynamic_update_slice x4, local copies, waits for them, and re-layouts, attend_backward(): lax.scan(one_block, (zeros_init, zeros_init), (query_blocks, grad_blocks,...  21.8 us
  transfers between devices with their start and end apart: 8, of which 2 were waited for; matrix products, arithmetic and copies ran while one was open for 25% of the time, Pallas kernels for 47%

profile of v3, /device:TPU:9, one launch (start us, length us, event | category | flops | bytes accessed | tf_op | source)
XLA Modules:
  0.0 650.4 jit_solution(5961678724226585173)
XLA Ops:
  10.7 49.0 %shard_map.204 = bf16[1024,1024]{1,0:T(8,128)(2,1)} custom-call(bf16[256,1024]{1,0:T(8,128)(2,1)} %bitcast.213), custom_call_target="tpu_custom_call" | custom-call | bytes 104857600 | tf_op jit(solution)/shard_map/pallas_call | solution.py:207
  59.7 5.5 shard_map.203
  65.3 5.1 all-to-all-start
  74.5 3.3 convolution_convert_fusion.6
  83.5 23.9 %while.27 = (s32[]{:T(128)}, bf16[2,512,4,64]{1,3,2,0:T(8,128)(2,1)}, f32[2,4,512]{2,1,0:T(4,128)S(1)}, s32[2]{0:T(128)S(1)}, s32[1024]{0:T(1024)S(1)}, /*index=...) while((s32[]{:T(128)}, ...), condition=%wide.region_7.8_spmd, body=%wide.region_4.7_spmd.sunk | while | flops 565312512 | bytes 33111280 | solution.py:114
  112.7 16.7 %shard_map.205 = bf16[256,1024]{1,0:T(8,128)(2,1)} custom-call(bf16[1024,256]{1,0:T(8,128)(2,1)} %reshape.602.part_ref), custom_call_target="tpu_custom_call" | custom-call | bytes 26214400 | tf_op jit(solution)/shard_map/pallas_call | solution.py:410
  133.4 4.8 all-to-all-start.1
  139.1 37.5 %shard_map.206 = bf16[1024,1024]{1,0:T(8,128)(2,1)} custom-call(bf16[256,1024]{1,0:T(8,128)(2,1)} %multiply_convert_fusion.9.own_ref), custom_call_target="tpu_custom_call" | custom-call | bytes 52428800 | tf_op jit(solution)/shard_map/pallas_call | solution.py:273
  176.6 6.9 %fusion.71 = f32[1024,2048]{1,0:T(8,128)S(1)} fusion(bf16[1024,1024]{1,0:T(8,128)(2,1)} %shard_map.206, bf16[1024,2048]{1,0:T(8,128)(2,1)} %bitcast.20), kind=kOutput, calls=%fused_computation.181 | convolution fusion | flops 4294967296 | bytes 14680064 | tf_op jit(solution)/shard_map/dot_general | solution.py:591
  189.1 5.9 convolution_convert_fusion.3
  194.9 18.0 %shard_map.207 = f32[256,1024]{1,0:T(8,128)} custom-call(bf16[4,256,1024]{2,1,0:T(8,128)(2,1)} %bitcast.218), custom_call_target="tpu_custom_call" | custom-call | bytes 52428800 | tf_op jit(solution)/shard_map/pallas_call | solution.py:351
  220.1 17.9 %shard_map.208 = bf16[1024,1024]{1,0:T(8,128)(2,1)} custom-call(bf16[256,1024]{1,0:T(8,128)(2,1)} %multiply_convert_fusion.5.own_ref), custom_call_target="tpu_custom_call" | custom-call | bytes 52428800 | tf_op jit(solution)/shard_map/pallas_call | solution.py:273
  238.0 9.8 %multiply_reduce_fusion.1 = (f32[1024]{0:T(1024)}, f32[1024]{0:T(1024)}, f32[1024,1024]{1,0:T(8,128)S(1)}, bf16[1024,1024]{1,0:T(8,128)(2,1)S(1)}) fusion(f32[1024,2048]{1,0:T(8,128)} %copy-done.16, f32[1024]{0:T(1024)S(1)} %bitcast.241, f32[1024]{0:T(1024)S(1)} %bitcast.244, bf16[1024,1024]{1,0:T(8,128)(2,1)} %shard_map.208, bf16[1024,1024]{1,0:T(8,128)(2,1)} %bitcast.23), kind=kOutput, calls=%fused_computation.62 | convolution fusion | flops 2167404544 | bytes 18890752 | tf_op jit(solution)/shard_map/dot_general | solution.py:39
  251.8 5.2 convolution_convert_fusion
  257.0 7.9 %fusion.49 = bf16[1024,1024]{1,0:T(8,128)(2,1)} fusion(bf16[1024,2048]{1,0:T(8,128)(2,1)} %bitcast.20, bf16[1024,1024]{1,0:T(8,128)(2,1)S(1)} %multiply_convert_fusion.1, bf16[1024,1024]{1,0:T(8,128)(2,1)S(1)} %get-tuple-element.336), kind=kOutput, calls=%fused_computation.76 | convolution fusion | flops 4304404480 | bytes 10485760 | tf_op jit(solution)/shard_map/dot_general | solution.py:39
  265.4 6.6 %pad_maximum_fusion = bf16[8,384,1024]{2,1,0:T(8,128)(2,1)} fusion(bf16[8,128,1024]{2,1,0:T(8,128)(2,1)S(1)} %bitcast.222, bf16[8,128,1024]{2,1,0:T(8,128)(2,1)S(1)} %bitcast.211, bf16[8,128,1024]{2,1,0:T(8,128)(2,1)S(1)} %bitcast.210), kind=kLoop, calls=%fused_computation.60 | loop fusion | flops 18874368 | bytes 12582912 | tf_op jit(solution)/shard_map/concatenate | solution.py:623
  272.1 5.3 all-to-all-start.3
  277.3 82.2 %shard_map.209 = f32[256,1024]{1,0:T(8,128)} custom-call(bf16[4,256,1024]{2,1,0:T(8,128)(2,1)} %bitcast.217), custom_call_target="tpu_custom_call" | custom-call | bytes 52428800 | tf_op jit(solution)/shard_map/pallas_call | solution.py:351
  371.2 16.7 %shard_map.210 = bf16[1024,256]{1,0:T(8,128)(2,1)} custom-call(bf16[256,1024]{1,0:T(8,128)(2,1)} %fusion.56.part_ref), custom_call_target="tpu_custom_call" | custom-call | bytes 26214400 | tf_op jit(solution)/shard_map/pallas_call | solution.py:410
  392.9 68.6 %while.28 = (s32[]{:T(128)}, f32[1024,4,64]{0,2,1:T(8,128)S(1)}, f32[1024,4,64]{0,2,1:T(8,128)}, f32[2,512,4,64]{1,0,3,2:T(2,128)}, bf16[2,512,4,64]{1,3,2,0:T(8...) while((s32[]{:T(128)}, f32[1024,4,64]{0,2,1:T(8,128)S(1)}, ...), condition=%wide.region_18.19_spmd.clone, body=%wide.region_16.18_spmd.clone.sunk | while | flops 1378221056 | bytes 164699536 | solution.py:160
  407.9 10.4 %dynamic_update_slice.32 = f32[2,512,4,64]{1,0,3,2:T(2,128)} dynamic-update-slice(f32[2,512,4,64]{1,0,3,2:T(2,128)} %get-tuple-element.570, f32[1,512,4,64]{1,0,3,2:T(1,128)S(1)} %copy.104, s32[]{:T(128)} %get-tuple-element.567, s32[]{:T(128)} %constant.63.clone.1..sunk.1, s32[]{:T(128)} %constant.63.clone.1..sunk.1, s32[]{:T(128)} %constant.63.clone.1..sunk.1) | dynamic-update-slice | bytes 1048580 | tf_op jit(solution)/shard_map/while/body/jit(dynamic_update_index_in_dim)/dynamic_update_slice | solution.py:160
  418.3 3.3 fusion.134
  423.0 3.5 fusion.135
  441.5 10.4 %dynamic_update_slice.32 = f32[2,512,4,64]{1,0,3,2:T(2,128)} dynamic-update-slice(f32[2,512,4,64]{1,0,3,2:T(2,128)} %get-tuple-element.570, f32[1,512,4,64]{1,0,3,2:T(1,128)S(1)} %copy.104, s32[]{:T(128)} %get-tuple-element.567, s32[]{:T(128)} %constant.63.clone.1..sunk.1, s32[]{:T(128)} %constant.63.clone.1..sunk.1, s32[]{:T(128)} %constant.63.clone.1..sunk.1) | dynamic-update-slice | bytes 1048580 | tf_op jit(solution)/shard_map/while/body/jit(dynamic_update_index_in_dim)/dynamic_update_slice | solution.py:160
  456.6 4.6 fusion.135
  467.0 3.5 add_reduce_fusion
  482.3 5.0 reduce_sum.209
  490.0 3.6 pad_maximum_fusion.2
  493.7 28.6 %reduce-scatter.4.cloned.1.call-done = bf16[160,768]{1,0:T(8,128)(2,1)} async-done(((bf16[1280,768]{1,0:T(8,128)(2,1)}), bf16[160,768]{1,0:T(8,128)(2,1)}) %reduce-scatter.4.cloned.1.call-update) | async-done | bytes 245776 | tf_op jit(solution)/shard_map/reduce_scatter | solution.py:713
  522.2 4.7 all-to-all-start.2
  527.0 4.6 convolution_convert_fusion.4
  531.6 99.2 %shard_map.211 = f32[256,1024]{1,0:T(8,128)} custom-call(bf16[4,256,1024]{2,1,0:T(8,128)(2,1)} %bitcast.219, f32[256,1024]{1,0:T(8,128)} %get-tuple-element.328.base_ref), custom_call_target="tpu_custom_call" | custom-call | bytes 104857600 | tf_op jit(solution)/shard_map/pallas_call | solution.py:456
  (288 shorter events, 141.4 us)
Async XLA Ops:
  7.2 67.4 %all-gather.2.cloned.1.call-start = ((), (), s32[]{:S(2)}) async-start(), calls=%async_computation.7 | async-start | bytes 4128768 | tf_op jit(solution)/shard_map/all_gather | solution.py:548
  65.2 7.5 %copy-start.43 = (f32[1024]{0:T(1024)S(1)}, f32[1024]{0:T(1024)}, u32[]{:S(2)}) copy-start(f32[1024]{0:T(1024)} %param.26) | copy-start | bytes 12292
  65.2 7.5 %copy-start.50 = (f32[1024]{0:T(1024)S(1)}, f32[1024]{0:T(1024)}, u32[]{:S(2)}) copy-start(f32[1024]{0:T(1024)} %param.25) | copy-start | bytes 12292
  65.2 9.3 %copy-start.27 = (bf16[1024,1024]{1,0:T(8,128)(2,1)S(1)}, bf16[1024,1024]{1,0:T(8,128)(2,1)}, u32[]{:S(2)}) copy-start(bf16[1024,1024]{1,0:T(8,128)(2,1)} %shard_map.204) | copy-start | bytes 6291460
  65.3 68.2 %all-to-all-start = ((bf16[8,128,2048]{2,1,0:T(8,128)(2,1)}), bf16[8,128,2048]{2,1,0:T(8,128)(2,1)}, u32[]{:S(2)}, u32[]{:S(2)}) async-start(bf16[8,128,2048]{2,1,0:T(8,128)(2,1)} %get-tuple-element.132), calls=%async_computation | async-start | bytes 8388608 | tf_op jit(solution)/shard_map/all_to_all | solution.py:558
  71.8 9.8 %copy-start.48 = (f32[4,64]{1,0:T(4,128)}, f32[4,64]{1,0:T(4,128)S(1)}, u32[]{:S(2)}) copy-start(f32[4,64]{1,0:T(4,128)S(1)} %mul.500) | copy-start | bytes 3076
  107.4 24.5 %copy-start.5 = (bf16[1024,4,64]{0,2,1:T(8,128)(2,1)}, bf16[1024,4,64]{0,2,1:T(8,128)(2,1)S(1)}, u32[]{:S(2)}) copy-start(bf16[1024,4,64]{0,2,1:T(8,128)(2,1)S(1)} %get-tuple-element.627) | copy-start | bytes 1572868
  107.4 25.5 %copy-start.23 = (bf16[1,256,1024]{2,1,0:T(8,128)(2,1)S(1)}, bf16[1,256,1024]{2,1,0:T(8,128)(2,1)}, u32[]{:S(2)}) copy-start(bf16[1,256,1024]{2,1,0:T(8,128)(2,1)} %param.16) | copy-start | bytes 1572868
  133.4 55.6 %all-to-all-start.1 = ((bf16[8,128,1024]{2,1,0:T(8,128)(2,1)}), bf16[8,128,1024]{2,1,0:T(8,128)(2,1)}, u32[]{:S(2)}, u32[]{:S(2)}) async-start(bf16[8,128,1024]{2,1,0:T(8,128)(2,1)} %get-tuple-element.133), calls=%async_computation.1 | async-start | bytes 4194304 | tf_op jit(solution)/shard_map/all_to_all | solution.py:559
  238.0 9.8 %copy-start.30 = (bf16[1024,1024]{1,0:T(8,128)(2,1)S(1)}, bf16[1024,1024]{1,0:T(8,128)(2,1)}, u32[]{:S(2)}) copy-start(bf16[1024,1024]{1,0:T(8,128)(2,1)} %shard_map.208) | copy-start | bytes 6291460
  238.0 9.8 %copy-start.32 = (bf16[1024,1024]{1,0:T(8,128)(2,1)S(1)}, bf16[1024,1024]{1,0:T(8,128)(2,1)}, u32[]{:S(2)}) copy-start(bf16[1024,1024]{1,0:T(8,128)(2,1)} %multiply_convert_fusion.3) | copy-start | bytes 6291460
  272.1 87.5 %copy-start.51 = (f32[1024]{0:T(1024)S(1)}, f32[1024]{0:T(1024)}, u32[]{:S(2)}) copy-start(f32[1024]{0:T(1024)} %get-tuple-element.371) | copy-start | bytes 12292
  272.1 210.2 %all-to-all-start.3 = ((bf16[8,384,1024]{2,1,0:T(8,128)(2,1)}), bf16[8,384,1024]{2,1,0:T(8,128)(2,1)}, u32[]{:S(2)}, u32[]{:S(2)}) async-start(bf16[8,384,1024]{2,1,0:T(8,128)(2,1)} %pad_maximum_fusion), calls=%async_computation.4 | async-start | bytes 12582912 | tf_op jit(solution)/shard_map/all_to_all | solution.py:631
  277.3 84.6 %copy-start.52 = (f32[1024]{0:T(1024)S(1)}, f32[1024]{0:T(1024)}, u32[]{:S(2)}) copy-start(f32[1024]{0:T(1024)} %get-tuple-element.370) | copy-start | bytes 12292
  277.3 212.7 %reduce-scatter.6.cloned.1.call-start = ((), (), s32[]{:S(2)}) async-start(), calls=%async_computation.9 | async-start | bytes 2359296 | tf_op jit(solution)/shard_map/reduce_scatter | solution.py:650
  367.9 25.0 %copy-start.3 = (f32[1024,4,64]{0,2,1:T(8,128)S(1)}, f32[1024,4,64]{0,2,1:T(8,128)}, u32[]{:S(2)}) copy-start(f32[1024,4,64]{0,2,1:T(8,128)} %custom-call) | copy-start | bytes 3145732
  367.9 25.0 %copy-start.6 = (bf16[1024,4,64]{0,2,1:T(8,128)(2,1)S(1)}, bf16[1024,4,64]{0,2,1:T(8,128)(2,1)}, u32[]{:S(2)}) copy-start(bf16[1024,4,64]{0,2,1:T(8,128)(2,1)} %copy-done.5) | copy-start | bytes 1572868
  367.9 154.4 %reduce-scatter.4.cloned.1.call-start = ((), (), s32[]{:S(2)}) async-start(), calls=%async_computation.8 | async-start | bytes 2211840 | tf_op jit(solution)/shard_map/reduce_scatter | solution.py:713
  392.9 71.9 %copy-start.45 = (f32[2,512,4]{1,0,2:T(2,128)S(1)}, f32[2,512,4]{1,0,2:T(2,128)}, u32[]{:S(2)}) copy-start(f32[2,512,4]{1,0,2:T(2,128)} %copy-done.44) | copy-start | bytes 49156
  392.9 71.9 %copy-start.49 = (f32[4,64]{1,0:T(4,128)S(1)}, f32[4,64]{1,0:T(4,128)}, u32[]{:S(2)}) copy-start(f32[4,64]{1,0:T(4,128)} %copy-done.48) | copy-start | bytes 3076
  461.5 5.5 copy-start.10
  461.5 5.5 copy-start.12
  461.5 5.5 copy-start.18
  461.5 5.5 copy-start.20
  461.6 5.5 copy-start.42
  461.6 5.5 copy-start.47
  464.8 6.2 copy-start.54
  464.8 6.3 copy-start.53
  482.2 153.7 %reduce-scatter.8.cloned.1.call-start = ((), (), s32[]{:S(2)}) async-start(), calls=%async_computation.10 | async-start | bytes 4259840 | tf_op jit(solution)/shard_map/reduce_scatter | solution.py:653
  490.0 37.0 %copy-start.34 = (bf16[1024,3,4,64]{0,3,2,1:T(8,128)(2,1)S(1)}, bf16[1024,3,4,64]{0,3,2,1:T(8,128)(2,1)}, u32[]{:S(2)}) copy-start(bf16[1024,3,4,64]{0,3,2,1:T(8,128)(2,1)} %copy-done.33) | copy-start | bytes 4718596
  522.2 108.6 %all-to-all-start.2 = ((bf16[4,40,768]{2,1,0:T(8,128)(2,1)}), bf16[4,40,768]{2,1,0:T(8,128)(2,1)S(1)}, u32[]{:S(2)}, u32[]{:S(2)}) async-start(bf16[4,40,768]{2,1,0:T(8,128)(2,1)} %bitcast.238), calls=%async_computation.3 | async-start | bytes 491520 | tf_op jit(solution)/shard_map/all_to_all | solution.py:723
  633.5 9.1 %copy-start.26 = (f32[256,1024]{1,0:T(8,128)S(1)}, f32[256,1024]{1,0:T(8,128)}, u32[]{:S(2)}) copy-start(f32[256,1024]{1,0:T(8,128)} %shard_map.211) | copy-start | bytes 3145732
  (39 other events, 125.7 us)
Sparse Core Ops, SparseCore 0:
  10.8 35.9 all-gather.1
  368.0 41.2 reduce-scatter.5
  482.4 39.8 reduce-scatter.3
  524.4 111.4 reduce-scatter.7

commit v4 on v3

--- a/solution.py
+++ b/solution.py
@@ -77,90 +77,134 @@
     return rotate(grad_rot, cosine, -sine_tab)
 
 
-def allowed(seg_row, block_start, block_len):
-    query_idx = block_start + jnp.arange(block_len, dtype=jnp.int32)
-    key_idx = jnp.arange(seg_row.shape[0], dtype=jnp.int32)
-    seg_query = lax.dynamic_slice_in_dim(seg_row, block_start, block_len)
-    same_doc = seg_query[:, None] == seg_row[None, :]
-    causal = key_idx[None, :] <= query_idx[:, None]
-    not_padding = (seg_query[:, None] != 0) | (key_idx[None, :] == query_idx[:, None])
-    return causal & same_doc & not_padding
+QUERY_BLOCK = 256
+
+
+def block_probs(query_part, key_part, key_seg, query_seg, first, score_scale):
+    rows = query_part.shape[0]
+    span = key_part.shape[0]
+    scores = contract_cols(key_part, query_part) * score_scale
+    key_idx = lax.broadcasted_iota(jnp.int32, (span, rows), 0)
+    query_idx = first + lax.broadcasted_iota(jnp.int32, (span, rows), 1)
+    open_seg = jnp.where(query_seg == 0, -1, query_seg)
+    allowed = ((key_seg == open_seg) & (key_idx <= query_idx)) | (key_idx == query_idx)
+    scores = jnp.where(allowed, scores, MASKED_SCORE)
+    weights_exp = jnp.exp(scores - jnp.max(scores, axis=0, keepdims=True))
+    return weights_exp * (1.0 / jnp.sum(weights_exp, axis=0, keepdims=True))
+
+
+def flip_f32(values):
+    return values.astype(jnp.float32).T
+
+
+def attn_forward_kernel(score_scale, query_ref, key_ref, value_ref, col_ref, row_ref, out_ref):
+    length, width = query_ref.shape
+    for head in range(width // HD):
+        lanes = slice(head * HD, (head + 1) * HD)
+        key_all = key_ref[:, lanes]
+        value_t = flip_f32(value_ref[:, lanes]).astype(jnp.bfloat16)
+        for first in range(0, length, QUERY_BLOCK):
+            span = first + QUERY_BLOCK
+            probs = block_probs(
+                query_ref[first:span, lanes],
+                key_all[:span],
+                col_ref[:span],
+                row_ref[:, first:span],
+                first,
+                score_scale,
+            ).astype(jnp.bfloat16)
+            mixed = jnp.dot(value_t[:, :span], probs, preferred_element_type=jnp.float32)
+            out_ref[first:span, lanes] = mixed.T.astype(out_ref.dtype)
+
+
+def attn_backward_kernel(
+    score_scale,
+    query_ref,
+    key_ref,
+    value_ref,
+    grad_ref,
+    col_ref,
+    row_ref,
+    query_out,
+    key_out,
+    value_out,
+):
+    length, width = query_ref.shape
+    for head in range(width // HD):
+        lanes = slice(head * HD, (head + 1) * HD)
+        key_all = key_ref[:, lanes]
+        value_all = value_ref[:, lanes]
+        key_t = flip_f32(key_all).astype(jnp.bfloat16)
+        for first in range(length - QUERY_BLOCK, -1, -QUERY_BLOCK):
+            span = first + QUERY_BLOCK
+            query_part = query_ref[first:span, lanes]
+            grad_part = grad_ref[first:span, lanes]
+            probs = block_probs(
+                query_part,
+                key_all[:span],
+                col_ref[:span],
+                row_ref[:, first:span],
+                first,
+                score_scale,
+            )
+            grad_value = jnp.dot(
+                probs.astype(jnp.bfloat16), grad_part, preferred_element_type=jnp.float32
+            )
+            grad_probs = contract_cols(value_all[:span], grad_part)
+            delta = jnp.sum(grad_probs * probs, axis=0, keepdims=True)
+            grad_scores = (probs * (grad_probs - delta)).astype(jnp.bfloat16)
+            grad_key = (
+                jnp.dot(grad_scores, query_part, preferred_element_type=jnp.float32) * score_scale
+            )
+            grad_query = (
+                jnp.dot(key_t[:, :span], grad_scores, preferred_element_type=jnp.float32)
+                * score_scale
+            )
+            query_out[first:span, lanes] = grad_query.T
+            if span == length:
+                key_out[:, lanes] = grad_key
+                value_out[:, lanes] = grad_value
+            else:
+                key_out[:span, lanes] += grad_key
+                value_out[:span, lanes] += grad_value
+
+
+def attn_call(kernel, score_scale, arrays, seg_row, outs):
+    length, width = arrays[0].shape
+    pair = min(2 * HD, width)
+    block = pl.BlockSpec((length, pair), lambda i: (0, i))
+    work = length * length * width
+    return pl.pallas_call(
+        functools.partial(kernel, score_scale),
+        grid=(width // pair,),
+        out_shape=[jax.ShapeDtypeStruct((length, width), dtype) for dtype in outs],
+        in_specs=[block] * len(arrays)
+        + [
+            pl.BlockSpec((length, 1), lambda i: (0, 0)),
+            pl.BlockSpec((1, length), lambda i: (0, 0)),
+        ],
+        out_specs=[block] * len(outs),
+        cost_estimate=pl.CostEstimate(
+            flops=24 * work * len(outs), bytes_accessed=8 * length * width, transcendentals=0
+        ),
+        compiler_params=pltpu.CompilerParams(vmem_limit_bytes=48 << 20),
+    )(*arrays, seg_row.reshape(length, 1), seg_row.reshape(1, length))
 
 
 def attend_forward(query_n, key_n, value_b, seg_row, score_scale):
-    length, groups, head_dim = query_n.shape
-    block_len = min(512, length)
-    block_count = length // block_len
-    query_blocks = query_n.reshape(block_count, block_len, groups, head_dim)
-    starts = jnp.arange(block_count, dtype=jnp.int32) * block_len
-
-    def one_block(block_in):
-        query_part, block_start = block_in
-        scores = (
-            jnp.einsum("qhd,khd->hqk", query_part, key_n, preferred_element_type=jnp.float32)
-            * score_scale
-        )
-        mask_ok = allowed(seg_row, block_start, block_len)
-        scores = jnp.where(mask_ok[None], scores, MASKED_SCORE)
-        row_max = jnp.max(scores, axis=-1, keepdims=True)
-        weights_exp = jnp.exp(scores - row_max)
-        row_total = jnp.sum(weights_exp, axis=-1, keepdims=True)
-        attn_probs = (weights_exp / row_total).astype(jnp.bfloat16)
-        attn_part = jnp.einsum(
-            "hqk,khd->qhd", attn_probs, value_b, preferred_element_type=jnp.float32
-        )
-        return (attn_part.astype(jnp.bfloat16), (row_max + jnp.log(row_total))[..., 0])
-
-    attn_mixed, log_sums = lax.map(one_block, (query_blocks, starts))
-    return (attn_mixed.reshape(length, groups * head_dim), log_sums)
-
-
-def attend_backward(query_n, key_n, value_b, grad_attn, log_sums, seg_row, score_scale):
-    length, groups, head_dim = query_n.shape
-    block_len = min(512, length)
-    block_count = length // block_len
-    query_blocks = query_n.reshape(block_count, block_len, groups, head_dim)
-    grad_blocks = grad_attn.reshape(block_count, block_len, groups, head_dim)
-    starts = jnp.arange(block_count, dtype=jnp.int32) * block_len
-
-    def one_block(accums, block_in):
-        key_acc, value_acc = accums
-        query_part, grad_part, lse_part, block_start = block_in
-        scores = (
-            jnp.einsum("qhd,khd->hqk", query_part, key_n, preferred_element_type=jnp.float32)
-            * score_scale
-        )
-        mask_ok = allowed(seg_row, block_start, block_len)
-        attn_probs = jnp.where(mask_ok[None], jnp.exp(scores - lse_part[..., None]), 0.0)
-        grad_probs = jnp.einsum(
-            "qhd,khd->hqk", grad_part, value_b, preferred_element_type=jnp.float32
-        )
-        delta_row = jnp.sum(grad_probs * attn_probs, axis=-1, keepdims=True)
-        grad_scores = (attn_probs * (grad_probs - delta_row)).astype(jnp.bfloat16)
-        grad_query = (
-            jnp.einsum("hqk,khd->qhd", grad_scores, key_n, preferred_element_type=jnp.float32)
-            * score_scale
-        )
-        key_acc = (
-            key_acc
-            + jnp.einsum(
-                "hqk,qhd->khd", grad_scores, query_part, preferred_element_type=jnp.float32
-            )
-            * score_scale
-        )
-        value_acc = value_acc + jnp.einsum(
-            "hqk,qhd->khd",
-            attn_probs.astype(jnp.bfloat16),
-            grad_part,
-            preferred_element_type=jnp.float32,
-        )
-        return ((key_acc, value_acc), grad_query)
-
-    zeros_init = jnp.zeros((length, groups, head_dim), jnp.float32)
-    (grad_key, grad_value), grad_query = lax.scan(
-        one_block, (zeros_init, zeros_init), (query_blocks, grad_blocks, log_sums, starts)
-    )
-    return (grad_query.reshape(length, groups, head_dim), grad_key, grad_value)
+    return attn_call(
+        attn_forward_kernel, score_scale, (query_n, key_n, value_b), seg_row, (jnp.bfloat16,)
+    )[0]
+
+
+def attend_backward(query_n, key_n, value_b, grad_attn, seg_row, score_scale):
+    return attn_call(
+        attn_backward_kernel,
+        score_scale,
+        (query_n, key_n, value_b, grad_attn),
+        seg_row,
+        (jnp.float32,) * 3,
+    )
 
 
 def greet(peers):
@@ -579,8 +623,10 @@
     key_unit, key_inv, key_n = head_prep(
         by_heads[:, 1].reshape(length, head_group, HD), cosine, sine_tab, head_gain
     )
-    value_b = by_heads[:, 2].reshape(length, head_group, HD)
-    attn_mixed, log_sums = attend_forward(query_n, key_n, value_b, seg_row, score_scale)
+    query_n = query_n.reshape(length, group_width)
+    key_n = key_n.reshape(length, group_width)
+    value_b = by_heads[:, 2]
+    attn_mixed = attend_forward(query_n, key_n, value_b, seg_row, score_scale)
     attn_pieces = seq_swap(attn_mixed, True)
     attn_proj = jnp.dot(attn_pieces, full_out, preferred_element_type=jnp.float32)
     attn_unit, attn_inv = rms_norm(attn_proj)
@@ -617,7 +663,6 @@
     ).astype(jnp.bfloat16)
     hidden_part = contract_cols(grad_up_gate, team_in)
     hidden_sum = team_sum(hidden_part.astype(jnp.bfloat16).reshape(TEAM, local_rows, model_width))
-    grad_hidden = (1.0 - alpha_mlp) * grad_two + hidden_sum
     in_terms = contract_rows(team_hidden, grad_up_gate).astype(jnp.bfloat16)
     down_terms = contract_rows(inner_act, team_grad).astype(jnp.bfloat16)
     ff_terms = jnp.concatenate(
@@ -628,6 +673,8 @@
         ],
         axis=1,
     )
+    ff_terms, hidden_sum = lax.optimization_barrier((ff_terms, hidden_sum))
+    grad_hidden = (1.0 - alpha_mlp) * grad_two + hidden_sum
     ff_terms = lax.all_to_all(ff_terms, "dp", 0, 0, tiled=True)
     ff_sums = jnp.sum(
         ff_terms.reshape(dp_count // TEAM, TEAM, 3, in_rows, model_width).astype(jnp.float32),
@@ -666,10 +713,13 @@
     )
     shard_w_down = shards[in_span:-out_rows].astype(jnp.float32)
     shard_w_attn_out = shards[-out_rows:].astype(jnp.float32)
-    grad_heads = seq_swap(grad_pieces, False).reshape(length, head_group, HD)
+    grad_heads = seq_swap(grad_pieces, False)
     grad_query_n, grad_key_n, grad_value = attend_backward(
-        query_n, key_n, value_b, grad_heads, log_sums, seg_row, score_scale
-    )
+        query_n, key_n, value_b, grad_heads, seg_row, score_scale
+    )
+    grad_query_n = grad_query_n.reshape(length, head_group, HD)
+    grad_key_n = grad_key_n.reshape(length, head_group, HD)
+    grad_value = grad_value.reshape(length, head_group, HD)
     grad_head_gain = jnp.sum(grad_query_n * query_unit + grad_key_n * key_unit, axis=0)
     grad_query = head_back(grad_query_n, query_unit, query_inv, head_gain, cosine, sine_tab)
     grad_key = head_back(grad_key_n, key_unit, key_inv, head_gain, cosine, sine_tab)

time: 663 us -> 538 us (0.81)
  Pallas kernels: 343 us -> 303 us
  matrix products: 91.7 us -> 58.1 us
  local copies, waits for them, and re-layouts: 71.8 us -> 42.2 us
  other arithmetic: 69.6 us -> 49.5 us
  waiting for transfers between devices: 31 us -> 39.9 us
  loops' own time: 8.48 us -> 0 us
    pallas_call x2, Pallas kernels: 100 us -> 36.3 us  [team_sum(): pl.pallas_call(team_sum_kernel, out_shape=jax.ShapeDtypeStruct((rows, wid...]
    dot_general x14 -> x0, matrix products: 35.9 us -> none  [the longest x2 8.03 us: one_block(): jnp.einsum('hqk,qhd->khd', attn_probs.astype(jnp.bfloat16), grad_part, pr...]
    pallas_call x0 -> x2, Pallas kernels: none -> 23.9 us  [attn_call(): pl.pallas_call(functools.partial(kernel, score_scale), grid=(width // pai...]
    dynamic_update_slice x4 -> x0, local copies, waits for them, and re-layouts: 21.8 us -> none  [attend_backward(): lax.scan(one_block, (zeros_init, zeros_init), (query_blocks, grad_blocks,...]
    all_to_all x1, waiting for transfers between devices: 0.01 us -> 16.3 us  [body(): ff_terms = lax.all_to_all(ff_terms, 'dp', 0, 0, tiled=True)]
    reshape x4 -> x0, local copies, waits for them, and re-layouts: 8.57 us -> none  [the longest x2 5.26 us: attend_forward(): return (attn_mixed.reshape(length, groups * head_dim), log_sums)]
    another operation x2 -> x0, loops' own time: 8.48 us -> none  [the longest x1 4.47 us: attend_backward(): lax.scan(one_block, (zeros_init, zeros_init), (query_blocks, grad_blocks,...]
    while x33 -> x0, local copies, waits for them, and re-layouts: 8.38 us -> none
  transfers between devices with their start and end apart: 8 -> 8, of which waited for: 2 -> 3; matrix products, arithmetic and copies ran while one was open for 25% -> 13% of each run, Pallas kernels for 47% -> 47%
where the time goes in v4:
time: 538 us; the launch traced here: 528 us
  Pallas kernels  303 us (56%)
  matrix products  58.1 us (11%)
  other arithmetic  49.5 us (9%)
  local copies, waits for them, and re-layouts  42.2 us (8%)
  waiting for transfers between devices  39.9 us (7%)
  starting transfers between devices  19.8 us (4%)
  between operations  15 us (3%)
    pallas_call x1, Pallas kernels, seq_sum(): pl.pallas_call(functools.partial(seq_sum_kernel, count), out_shape=jax.Sh...  99.3 us
    pallas_call x2, Pallas kernels, team_gather(): pl.pallas_call(team_gather_kernel, out_shape=jax.ShapeDtypeStruct((TEAM *...  55.2 us
    pallas_call x1, Pallas kernels, seq_gather(): pl.pallas_call(functools.partial(seq_gather_kernel, count), out_shape=jax...  49 us
    pallas_call x2, Pallas kernels, team_sum(): pl.pallas_call(team_sum_kernel, out_shape=jax.ShapeDtypeStruct((rows, wid...  36.3 us
    pallas_call x2, Pallas kernels, seq_swap(): pl.pallas_call(functools.partial(seq_swap_kernel, to_tokens, count), out_...  33.7 us
    dot_general x4, matrix products, contract_cols(): lax.dot_general(left_arr, right_arr, (((1,), (1,)), ((), ())), preferred_...  25.5 us
    pallas_call x2, Pallas kernels, attn_call(): pl.pallas_call(functools.partial(kernel, score_scale), grid=(width // pai...  23.9 us
    reduce_scatter x1, waiting for transfers between devices, body(): lax.psum_scatter(packed.reshape(dp_count * seq_count * span, 3 * group_wi...  21.1 us
  transfers between devices with their start and end apart: 8, of which 3 were waited for; matrix products, arithmetic and copies ran while one was open for 13% of the time, Pallas kernels for 47%

profile of v4, /device:TPU:9, one launch (start us, length us, event | category | flops | bytes accessed | tf_op | source)
XLA Modules:
  0.0 527.6 jit_solution(8569252153588402366)
XLA Ops:
  10.7 49.0 %shard_map.204 = bf16[1024,1024]{1,0:T(8,128)(2,1)} custom-call(bf16[256,1024]{1,0:T(8,128)(2,1)} %bitcast.117), custom_call_target="tpu_custom_call" | custom-call | bytes 104857600 | tf_op jit(solution)/shard_map/pallas_call | solution.py:251
  59.7 5.6 %shard_map.203 = (bf16[8,128,2048]{2,1,0:T(8,128)(2,1)}, bf16[8,128,1024]{2,1,0:T(8,128)(2,1)}) custom-call(bf16[128,8192]{1,0:T(8,128)(2,1)} %in_ref.1, bf16[512,1024]{1,0:T(8,128)(2,1)} %down_ref.1), custom_call_target="tpu_custom_call" | custom-call | bytes 8388608 | tf_op jit(solution)/shard_map/pallas_call | solution.py:535
  65.3 5.1 all-to-all-start
  74.2 3.3 convolution_convert_fusion.6
  87.0 9.5 %shard_map.205.part_ref = bf16[1024,256]{1,0:T(8,128)(2,1)S(1)} custom-call(bf16[1024,256]{1,0:T(8,128)(2,1)S(1)} %get-tuple-element.74.query_ref, bf16[1024,256]{1,0:T(8,128)(2,1)S(1)} %get-tuple-element.73.key_ref, bf16[1024,256]{1,0:T(8,128)(2,1)S(1)} %bitcast.106, s32[1024,1]{1,0:T(8,128)S(1)} %copy.73.col_ref, s32[1,1024]{1,0:T(1,128)S(1)} %copy-done.10), custom_call_target="tpu_custom_call" | custom-call | flops 6442450944 | bytes 2097152 | tf_op jit(solution)/shard_map/pallas_call | solution.py:177
  99.0 16.9 %shard_map.206 = bf16[256,1024]{1,0:T(8,128)(2,1)} custom-call(bf16[1024,256]{1,0:T(8,128)(2,1)} %copy-done.5), custom_call_target="tpu_custom_call" | custom-call | bytes 26214400 | tf_op jit(solution)/shard_map/pallas_call | solution.py:454
  115.9 2.6 multiply_reduce_fusion.12
  119.9 4.6 all-to-all-start.1
  125.6 37.3 %shard_map.207 = bf16[1024,1024]{1,0:T(8,128)(2,1)} custom-call(bf16[256,1024]{1,0:T(8,128)(2,1)} %multiply_convert_fusion.8.own_ref), custom_call_target="tpu_custom_call" | custom-call | bytes 52428800 | tf_op jit(solution)/shard_map/pallas_call | solution.py:317
  163.0 6.9 %fusion.25 = f32[1024,2048]{1,0:T(8,128)S(1)} fusion(bf16[1024,1024]{1,0:T(8,128)(2,1)} %shard_map.207, bf16[1024,2048]{1,0:T(8,128)(2,1)} %bitcast.16), kind=kOutput, calls=%fused_computation.119 | convolution fusion | flops 4294967296 | bytes 14680064 | tf_op jit(solution)/shard_map/dot_general | solution.py:637
  169.9 3.2 copy-done.22
  175.5 5.9 %convolution_convert_fusion.3 = bf16[1024,1024]{1,0:T(8,128)(2,1)} fusion(bf16[1024,1024]{1,0:T(8,128)(2,1)} %multiply_convert_fusion.2, bf16[1024,1024]{1,0:T(8,128)(2,1)} %bitcast.19), kind=kOutput, calls=%fused_computation.19 | convolution fusion | flops 2148532224 | bytes 6291456 | tf_op jit(solution)/shard_map/dot_general | solution.py:645
  181.4 18.1 %shard_map.208 = f32[256,1024]{1,0:T(8,128)} custom-call(bf16[4,256,1024]{2,1,0:T(8,128)(2,1)} %bitcast.122), custom_call_target="tpu_custom_call" | custom-call | bytes 52428800 | tf_op jit(solution)/shard_map/pallas_call | solution.py:395
  205.2 17.9 %shard_map.209 = bf16[1024,1024]{1,0:T(8,128)(2,1)} custom-call(bf16[256,1024]{1,0:T(8,128)(2,1)} %multiply_convert_fusion.4.own_ref), custom_call_target="tpu_custom_call" | custom-call | bytes 52428800 | tf_op jit(solution)/shard_map/pallas_call | solution.py:317
  223.1 9.0 %multiply_reduce_fusion = (f32[1024]{0:T(1024)S(1)}, f32[1024]{0:T(1024)S(1)}, f32[1024,1024]{1,0:T(8,128)S(1)}, bf16[1024,1024]{1,0:T(8,128)(2,1)S(1)}) fusion(f32[1024,2048]{1,0:T(8,128)} %copy-done.22, f32[1024]{0:T(1024)S(1)} %bitcast.137, f32[1024]{0:T(1024)S(1)} %bitcast.140, bf16[1024,1024]{1,0:T(8,128)(2,1)} %shard_map.209, ...), kind=kOutput, calls=%fused_computation.2 | convolution fusion | flops 2167404544 | bytes 18890752 | tf_op jit(solution)/shard_map/dot_general | solution.py:39
  232.8 8.5 %fusion.2 = bf16[1024,1024]{1,0:T(8,128)(2,1)} fusion(bf16[1024,2048]{1,0:T(8,128)(2,1)} %bitcast.16, bf16[1024,1024]{1,0:T(8,128)(2,1)S(1)} %multiply_convert_fusion, bf16[1024,1024]{1,0:T(8,128)(2,1)S(1)} %get-tuple-element.44), kind=kOutput, calls=%fused_computation.16 | convolution fusion | flops 4304404480 | bytes 10485760 | tf_op jit(solution)/shard_map/dot_general | solution.py:39
  241.3 6.3 %convolution_convert_fusion = bf16[1024,2048]{1,0:T(8,128)(2,1)} fusion(bf16[1024,1024]{1,0:T(8,128)(2,1)S(1)} %copy-done.28, bf16[1024,1024]{1,0:T(8,128)(2,1)S(1)} %multiply_convert_fusion, bf16[1024,1024]{1,0:T(8,128)(2,1)S(1)} %get-tuple-element.44), kind=kOutput, calls=%fused_computation.12 | convolution fusion | flops 4305453056 | bytes 10485760 | tf_op jit(solution)/shard_map/dot_general | solution.py:33
  247.6 3.7 convolution_convert_fusion.2
  251.3 18.3 %shard_map.210 = f32[256,1024]{1,0:T(8,128)} custom-call(bf16[4,256,1024]{2,1,0:T(8,128)(2,1)} %bitcast.121), custom_call_target="tpu_custom_call" | custom-call | bytes 52428800 | tf_op jit(solution)/shard_map/pallas_call | solution.py:395
  269.6 2.8 fusion.21
  272.5 6.8 %pad_maximum_fusion = bf16[8,384,1024]{2,1,0:T(8,128)(2,1)} fusion(bf16[8,128,1024]{2,1,0:T(8,128)(2,1)S(1)} %bitcast.127, bf16[8,128,1024]{2,1,0:T(8,128)(2,1)S(1)} %bitcast.115, bf16[8,128,1024]{2,1,0:T(8,128)(2,1)S(1)} %bitcast.114), kind=kLoop, calls=%fused_computation | loop fusion | flops 18874368 | bytes 12582912 | tf_op jit(solution)/shard_map/concatenate | solution.py:668
  285.1 5.3 %all-to-all-start.3 = ((bf16[8,384,1024]{2,1,0:T(8,128)(2,1)}), bf16[8,384,1024]{2,1,0:T(8,128)(2,1)}, u32[]{:S(2)}, u32[]{:S(2)}) async-start(bf16[8,384,1024]{2,1,0:T(8,128)(2,1)} %pad_maximum_fusion), calls=%async_computation.4 | async-start | bytes 12582912 | tf_op jit(solution)/shard_map/all_to_all | solution.py:678
  290.4 3.3 fusion.9.part_ref
  293.7 16.8 %shard_map.211.grad_ref = bf16[1024,256]{1,0:T(8,128)(2,1)} custom-call(bf16[256,1024]{1,0:T(8,128)(2,1)} %fusion.9.part_ref), custom_call_target="tpu_custom_call" | custom-call | bytes 26214400 | tf_op jit(solution)/shard_map/pallas_call | solution.py:454
  315.8 14.4 %shard_map.212 = (f32[1024,256]{1,0:T(8,128)S(1)}, f32[1024,256]{1,0:T(8,128)S(1)}, f32[1024,256]{1,0:T(8,128)S(1)}) custom-call(bf16[1024,256]{1,0:T(8,128)(2,1)S(1)} %copy-done.9, bf16[1024,256]{1,0:T(8,128)(2,1)S(1)} %copy-done.7, bf16[1024,256]{1,0:T(8,128)(2,1)S(1)} %bitcast.107, bf16[1024,256]{1,0:T(8,128)(2,1)S(1)} %copy-done.4, ...), custom_call_target="tpu_custom_call" | custom-call | flops 19327352832 | bytes 2097152 | tf_op jit(solution)/shard_map/pallas_call | solution.py:177
  350.6 16.3 %all-to-all-done.3 = bf16[8,384,1024]{2,1,0:T(8,128)(2,1)} async-done(((bf16[8,384,1024]{2,1,0:T(8,128)(2,1)}), bf16[8,384,1024]{2,1,0:T(8,128)(2,1)}, u32[]{:S(2)}, u32[]{:S(2)}) %all-to-all-start.3) | async-done | bytes 6291488 | tf_op jit(solution)/shard_map/all_to_all | solution.py:678
  366.9 5.3 %reduce_sum.191 = bf16[4,3,128,1024]{3,2,1,0:T(8,128)(2,1)S(1)} reduce(bf16[2,4,3,128,1024]{4,3,2,1,0:T(8,128)(2,1)} %bitcast.42, bf16[]{:T(256)} %constant.68.clone.1), dimensions={0}, to_apply=%region_20.21 | reduce | flops 1572864 | bytes 9437186 | tf_op jit(solution)/shard_map/reduce_sum | solution.py:679
  374.9 3.3 pad_maximum_fusion.2
  378.3 21.1 %reduce-scatter.4.cloned.1.call-done = bf16[160,768]{1,0:T(8,128)(2,1)} async-done(((bf16[1280,768]{1,0:T(8,128)(2,1)}), bf16[160,768]{1,0:T(8,128)(2,1)}) %reduce-scatter.4.cloned.1.call-update) | async-done | bytes 245776 | tf_op jit(solution)/shard_map/reduce_scatter | solution.py:763
  399.4 4.6 all-to-all-start.2
  404.0 4.6 convolution_convert_fusion.4
  408.6 99.3 %shard_map.213 = f32[256,1024]{1,0:T(8,128)} custom-call(bf16[4,256,1024]{2,1,0:T(8,128)(2,1)} %bitcast.123, f32[256,1024]{1,0:T(8,128)} %get-tuple-element.40.base_ref), custom_call_target="tpu_custom_call" | custom-call | bytes 104857600 | tf_op jit(solution)/shard_map/pallas_call | solution.py:500
  (199 shorter events, 76.8 us)
Async XLA Ops:
  7.2 67.0 %all-gather.2.cloned.1.call-start = ((), (), s32[]{:S(2)}) async-start(), calls=%async_computation.7 | async-start | bytes 4128768 | tf_op jit(solution)/shard_map/all_gather | solution.py:592
  65.3 5.1 copy-start.10
  65.3 7.7 %copy-start.40 = (f32[1024]{0:T(1024)S(1)}, f32[1024]{0:T(1024)}, u32[]{:S(2)}) copy-start(f32[1024]{0:T(1024)} %param.22) | copy-start | bytes 12292
  65.3 7.7 %copy-start.43 = (f32[1024]{0:T(1024)S(1)}, f32[1024]{0:T(1024)}, u32[]{:S(2)}) copy-start(f32[1024]{0:T(1024)} %param.21) | copy-start | bytes 12292
  65.3 8.9 %copy-start.26 = (bf16[1024,1024]{1,0:T(8,128)(2,1)S(1)}, bf16[1024,1024]{1,0:T(8,128)(2,1)}, u32[]{:S(2)}) copy-start(bf16[1024,1024]{1,0:T(8,128)(2,1)} %shard_map.204) | copy-start | bytes 6291460
  65.3 54.6 %all-to-all-start = ((bf16[8,128,2048]{2,1,0:T(8,128)(2,1)}), bf16[8,128,2048]{2,1,0:T(8,128)(2,1)}, u32[]{:S(2)}, u32[]{:S(2)}) async-start(bf16[8,128,2048]{2,1,0:T(8,128)(2,1)} %get-tuple-element.24), calls=%async_computation | async-start | bytes 8388608 | tf_op jit(solution)/shard_map/all_to_all | solution.py:602
  72.0 15.1 %copy-start = (s32[1024,1]{1,0:T(8,128)}, s32[1024,1]{1,0:T(8,128)S(1)}, u32[]{:S(2)}) copy-start(s32[1024,1]{1,0:T(8,128)S(1)} %copy.73.col_ref) | copy-start | bytes 12292
  74.2 4.5 copy-start.37
  79.8 4.1 copy-start.41
  80.0 3.9 copy-start.12
  81.4 5.7 %copy-start.42 = (f32[1024,4]{0,1:T(4,128)}, f32[1024,4]{0,1:T(4,128)S(1)}, u32[]{:S(2)}) copy-start(f32[1024,4]{0,1:T(4,128)S(1)} %add_rsqrt_fusion) | copy-start | bytes 49156
  82.5 14.0 %copy-start.14 = (f32[1024,4,64]{0,2,1:T(8,128)}, f32[1024,4,64]{0,2,1:T(8,128)S(1)}, u32[]{:S(2)}) copy-start(f32[1024,4,64]{0,2,1:T(8,128)S(1)} %fusion.14) | copy-start | bytes 3145732
  85.1 11.4 %copy-start.2 = (bf16[1024,1,256]{2,0,1:T(8,128)(2,1)}, bf16[1024,1,256]{2,0,1:T(8,128)(2,1)S(1)}, u32[]{:S(2)}) copy-start(bf16[1024,1,256]{2,0,1:T(8,128)(2,1)S(1)} %copy.83) | copy-start | bytes 1572868
  99.0 20.5 %copy-start.23 = (bf16[1,256,1024]{2,1,0:T(8,128)(2,1)S(1)}, bf16[1,256,1024]{2,1,0:T(8,128)(2,1)}, u32[]{:S(2)}) copy-start(bf16[1,256,1024]{2,1,0:T(8,128)(2,1)} %param.12) | copy-start | bytes 1572868
  119.9 55.6 %all-to-all-start.1 = ((bf16[8,128,1024]{2,1,0:T(8,128)(2,1)}), bf16[8,128,1024]{2,1,0:T(8,128)(2,1)}, u32[]{:S(2)}, u32[]{:S(2)}) async-start(bf16[8,128,1024]{2,1,0:T(8,128)(2,1)} %get-tuple-element.25), calls=%async_computation.1 | async-start | bytes 4194304 | tf_op jit(solution)/shard_map/all_to_all | solution.py:603
  124.5 250.4 %reduce-scatter.6.cloned.1.call-start = ((), (), s32[]{:S(2)}) async-start(), calls=%async_computation.9 | async-start | bytes 2359296 | tf_op jit(solution)/shard_map/reduce_scatter | solution.py:697
  169.9 3.2 copy-start.22
  181.4 21.2 %copy-start.16 = (bf16[1,256,1024]{2,1,0:T(8,128)(2,1)S(1)}, bf16[1,256,1024]{2,1,0:T(8,128)(2,1)}, u32[]{:S(2)}) copy-start(bf16[1,256,1024]{2,1,0:T(8,128)(2,1)} %param.23) | copy-start | bytes 1572868
  199.4 3.2 copy-start.11
  232.7 8.5 %copy-start.28 = (bf16[1024,1024]{1,0:T(8,128)(2,1)S(1)}, bf16[1024,1024]{1,0:T(8,128)(2,1)}, u32[]{:S(2)}) copy-start(bf16[1024,1024]{1,0:T(8,128)(2,1)} %shard_map.207) | copy-start | bytes 6291460
  241.3 6.3 %copy-start.29 = (bf16[1024,1024]{1,0:T(8,128)(2,1)S(1)}, bf16[1024,1024]{1,0:T(8,128)(2,1)}, u32[]{:S(2)}) copy-start(bf16[1024,1024]{1,0:T(8,128)(2,1)} %shard_map.209) | copy-start | bytes 6291460
  241.3 6.3 %copy-start.32 = (bf16[1024,1024]{1,0:T(8,128)(2,1)S(1)}, bf16[1024,1024]{1,0:T(8,128)(2,1)}, u32[]{:S(2)}) copy-start(bf16[1024,1024]{1,0:T(8,128)(2,1)} %multiply_convert_fusion.2) | copy-start | bytes 6291460
  272.5 6.8 %copy-start.17 = (f32[256,1024]{1,0:T(8,128)S(1)}, f32[256,1024]{1,0:T(8,128)}, u32[]{:S(2)}) copy-start(f32[256,1024]{1,0:T(8,128)} %shard_map.210) | copy-start | bytes 3145732
  285.1 81.8 %all-to-all-start.3 = ((bf16[8,384,1024]{2,1,0:T(8,128)(2,1)}), bf16[8,384,1024]{2,1,0:T(8,128)(2,1)}, u32[]{:S(2)}, u32[]{:S(2)}) async-start(bf16[8,384,1024]{2,1,0:T(8,128)(2,1)} %pad_maximum_fusion), calls=%async_computation.4 | async-start | bytes 12582912 | tf_op jit(solution)/shard_map/all_to_all | solution.py:678
  290.4 109.0 %reduce-scatter.4.cloned.1.call-start = ((), (), s32[]{:S(2)}) async-start(), calls=%async_computation.8 | async-start | bytes 2211840 | tf_op jit(solution)/shard_map/reduce_scatter | solution.py:763
  333.7 7.5 %copy-start.13 = (f32[1024,4,64]{0,2,1:T(8,128)S(1)}, f32[1024,4,64]{0,2,1:T(8,128)}, u32[]{:S(2)}) copy-start(f32[1024,4,64]{0,2,1:T(8,128)} %copy-done.12) | copy-start | bytes 3145732
  337.8 6.0 %copy-start.15 = (f32[1024,4,64]{0,2,1:T(8,128)S(1)}, f32[1024,4,64]{0,2,1:T(8,128)}, u32[]{:S(2)}) copy-start(f32[1024,4,64]{0,2,1:T(8,128)} %copy-done.14) | copy-start | bytes 3145732
  337.8 6.0 %copy-start.20 = (f32[1024,256]{0,1:T(8,128)S(1)}, f32[1024,256]{0,1:T(8,128)}, u32[]{:S(2)}) copy-start(f32[1024,256]{0,1:T(8,128)} %copy.75) | copy-start | bytes 3145732
  350.5 162.4 %reduce-scatter.8.cloned.1.call-start = ((), (), s32[]{:S(2)}) async-start(), calls=%async_computation.10 | async-start | bytes 4259840 | tf_op jit(solution)/shard_map/reduce_scatter | solution.py:700
  378.2 25.7 %copy-start.35 = (bf16[1024,3,4,64]{0,3,2,1:T(8,128)(2,1)S(1)}, bf16[1024,3,4,64]{0,3,2,1:T(8,128)(2,1)}, u32[]{:S(2)}) copy-start(bf16[1024,3,4,64]{0,3,2,1:T(8,128)(2,1)} %copy-done.34) | copy-start | bytes 4718596
  399.4 108.5 %all-to-all-start.2 = ((bf16[4,40,768]{2,1,0:T(8,128)(2,1)}), bf16[4,40,768]{2,1,0:T(8,128)(2,1)S(1)}, u32[]{:S(2)}, u32[]{:S(2)}) async-start(bf16[4,40,768]{2,1,0:T(8,128)(2,1)} %bitcast.135), calls=%async_computation.3 | async-start | bytes 491520 | tf_op jit(solution)/shard_map/all_to_all | solution.py:773
  514.1 5.6 %copy-start.25 = (f32[256,1024]{1,0:T(8,128)S(1)}, f32[256,1024]{1,0:T(8,128)}, u32[]{:S(2)}) copy-start(f32[256,1024]{1,0:T(8,128)} %shard_map.213) | copy-start | bytes 3145732
  (20 other events, 27.8 us)
Sparse Core Ops, SparseCore 0:
  10.8 35.9 all-gather.1
  285.2 65.8 reduce-scatter.5
  354.5 44.8 reduce-scatter.3
  401.6 111.2 reduce-scatter.7
